TPU v7x, 128 devices: a whole 4x4x4 slice. The times are simulated.
128 devices in a mesh: gx: 16 (over z_hi, y, core), gy: 8 (over x, z_lo).
Axes of the slice: x: 4, y: 4, z: 4 (z_hi: 2, z_lo: 2; z = z_hi * 2 + z_lo), core: 2. Of those that a mesh axis runs over, the one named last changes fastest.
Arguments:
- tracer_amounts: bfloat16 [2, 1024, 1024, 128], P(None, ('gx', 'gy')), may hold values from 0.099609375 to 3
- zonal_transit_ratio: float32 [2, 1024, 1024], P(None, 'gx', 'gy'), may hold values from -0.5 to 0.5
- meridional_transit_ratio: float32 [2, 1024, 1024], P(None, 'gx', 'gy'), may hold values from -0.45 to 0.45
- moisture_ratio: float32 [2, 1024, 1024], P(None, 'gx', 'gy'), may hold values from 0.2 to 0.9
- stratum_depths: float32 [2, 1024, 1024], P(None, 'gx', 'gy'), may hold values from 0.5 to 2
- sun_elevation_factor: float32 [1024, 1024], P('gx', 'gy'), may hold values from 0.2 to 1
- thermal_anomaly: float32 [2, 1024, 1024], P(None, 'gx', 'gy'), may hold values from -6 to 6
- particle_class_map: int32 [1024, 1024], P(('gx', 'gy')), may hold values from 0 to 7
- ground_cover_kind: int32 [1024, 1024], P(('gx', 'gy')), may hold values from 0 to 23
- arid_extinction_table: bfloat16 [128, 64], replicated, may hold values from 0 to 0.015625
- swelling_factors: bfloat16 [128, 64], replicated, may hold values from 0 to 0.00390625
- settling_velocities: float32 [24, 128], replicated, may hold values from 0.05 to 2
- arriving_irradiance: float32 [4], replicated, may hold values from 0.5 to 2
Outputs:
- updated_tracer_amounts: float32 [2, 1024, 1024, 128], P(None, ('gx', 'gy'))
- updated_thermal_anomaly: float32 [2, 1024, 1024], P(None, 'gx', 'gy')
All inputs are finite; a program needn't handle non-finite values.
Results may differ from a plain program's by a relative error of at most 0.00075.
Values may be sent and summed in bfloat16 or wider, within the bound.
No kernel may reach another device: no remote copies, remote signals or barrier semaphores. Data moves between devices by JAX's collectives and lax.ppermute only.
A program may use at most 128 MiB of HBM per device.

v0:
```python
import functools

import jax
import jax.numpy as jnp
import numpy as np
from jax import lax
from jax.experimental import pallas as pl
from jax.experimental.pallas import tpu as pltpu
from jax.sharding import PartitionSpec as P


SUB = 3
NBIN = 8
NW = 4
SPREAD_FACTOR = 0.2

LANES = 128
MARGIN = 16
RIM = 2
CHUNKS = (384, 256, 256, 128)

UV_ROWS = 24
MOIST_ROW = 48
DEPTH_ROW = 64
SUN_ROW = 80
EDGE_ROW = 88
FIELD_ROWS = 96


def spread_matrix():
    field = np.full((LANES,), -1)
    for k in range(72):
        field[k] = k % 24
    for k in range(24):
        field[72 + k] = 24 + k % 8
    field[96:104] = 32 + np.arange(8)
    out = np.zeros((20, LANES, 2 * LANES), np.float32)
    for k in range(LANES):
        if field[k] >= 0:
            half = field[k] % 2
            out[field[k] // 2, k, half * LANES : (half + 1) * LANES] = 1.0
    return out


def three_parts(x):
    high = x.astype(jnp.bfloat16).astype(jnp.float32)
    rest = x - high
    middle = rest.astype(jnp.bfloat16).astype(jnp.float32)
    return [high, middle, rest - middle]


def pack_kernel(place, u, v, moisture, depth, sun, warmth, low, high, out, ext):
    mine = place[0]
    parts = u.shape[1] // 8
    for f in range(4):
        source = (u, v)[f // 2]
        ext[f, 8 : 8 + u.shape[1], :] = source[f % 2]
        ext[f, 8 - RIM : 8, :] = low[RIM * f : RIM * (f + 1), :]
        ext[f, 8 + u.shape[1] : 8 + u.shape[1] + RIM, :] = high[RIM * f : RIM * (f + 1), :]
    turned = warmth[...].reshape(2 * u.shape[1], LANES).T
    last = turned[LANES - 1 :, :]
    initial = turned[:1, :]
    wide = 8 + 2 * RIM
    for d in range(parts):
        for level in range(2):
            base = UV_ROWS * level
            out[d, base : base + wide, :] = ext[level, 8 * d + 8 - RIM : 8 * d + 16 + RIM, :]
            out[d, base + wide : base + 2 * wide, :] = ext[
                2 + level, 8 * d + 8 - RIM : 8 * d + 16 + RIM, :
            ]
            out[d, MOIST_ROW + 8 * level : MOIST_ROW + 8 * level + 8, :] = moisture[
                level, 8 * d : 8 * d + 8, :
            ]
            out[d, DEPTH_ROW + 8 * level : DEPTH_ROW + 8 * level + 8, :] = depth[
                level, 8 * d : 8 * d + 8, :
            ]
        out[d, SUN_ROW : SUN_ROW + 8, :] = sun[8 * d : 8 * d + 8, :]
        row = jnp.where(mine + 1 == d, last, jnp.where(mine - 1 == d, initial, 0.0))
        out[d, EDGE_ROW : EDGE_ROW + 8, :] = jnp.broadcast_to(row, (8, LANES))


def warm_kernel(place, warmth, low, high, left, right, out, ext):
    span = warmth.shape[1]
    lane = lax.broadcasted_iota(jnp.int32, (span, LANES), 1)
    for level in range(2):
        here = warmth[level]
        ext[8 : 8 + span, :] = here
        ext[7:8, :] = low[level : level + 1, :]
        ext[8 + span : 9 + span, :] = high[level : level + 1, :]
        left_rows = jnp.broadcast_to(left[:, level * span : (level + 1) * span], (LANES, span)).T
        right_rows = jnp.broadcast_to(right[:, level * span : (level + 1) * span], (LANES, span)).T
        west = jnp.where(lane == 0, left_rows, pltpu.roll(here, 1, 1))
        east = jnp.where(lane == LANES - 1, right_rows, pltpu.roll(here, LANES - 1, 1))
        laplace = ext[9 : 9 + span, :] + ext[7 : 7 + span, :] + east + west - 4.0 * here
        out[level] = here + SPREAD_FACTOR * laplace


def row_blocks(first, count, size=64):
    blocks = []
    while count > 0:
        take = size if count >= 2 * size or count == size else min(count, 2 * size - 8)
        if take > size + 32:
            take = (take // 2 + 7) // 8 * 8
        blocks.append((first, take))
        first += take
        count -= take
    return blocks


def chunk_kernel(start, rows, grid_rows, first, final, *refs):
    refs = list(refs)
    zero, sunlight, fields, kind, bins, spread, table, speeds, tracer = refs[:9]
    del refs[:9]
    west, east = refs[:2]
    del refs[:2]
    if not first:
        west_before, east_before = refs[:2]
        del refs[:4]
    out, heat = refs[:2]
    even, odd, coef, turned, result, thick, warm, out_sems, heat_sem = refs[2:]

    stop = start + rows
    span = rows + 2 * MARGIN
    blocks = rows // LANES
    first_block = start // LANES
    low = 0 if first else start - MARGIN
    top = grid_rows if final else stop + MARGIN
    offset = low - (start - MARGIN)
    filled = top - low
    columns = 8
    wide = columns + 2 * SUB
    z = zero[0]

    sublane = lax.broadcasted_iota(jnp.int32, (8, LANES), 0)
    weights = jnp.zeros((8, LANES), jnp.float32)
    for w in range(NW):
        weights = jnp.where(sublane == NW + w, sunlight[w], weights)
    lane = lax.broadcasted_iota(jnp.int32, (1, LANES), 1)
    category = jnp.where(lane < 72, lane % 24, -1).astype(jnp.float32)

    def turn(block, level):
        parts = three_parts(fields[block, UV_ROWS * level : UV_ROWS * (level + 1), :])
        if level == 0:
            parts += three_parts(fields[block, DEPTH_ROW : DEPTH_ROW + 8, :])
            parts.append(kind[:, block * LANES : (block + 1) * LANES].astype(jnp.float32))
            parts.append(jnp.zeros((24, LANES), jnp.float32))
        else:
            parts.append(jnp.zeros((56, LANES), jnp.float32))
        return jnp.concatenate(parts, axis=0).T.astype(jnp.bfloat16)

    def row(block, at):
        return fields[block, at : at + 1, :]

    def step(source, c, i, r0, count):
        here = source[c, r0 : r0 + count, :]
        u = coef[i, r0 : r0 + count, :]
        v = coef[12 + i, r0 : r0 + count, :]
        across = jnp.where(
            u > 0.0, source[c - 1, r0 : r0 + count, :], source[c + 1, r0 : r0 + count, :]
        )
        along = jnp.where(
            v > 0.0,
            source[c, pl.ds(z + (r0 - 1), count), :],
            source[c, pl.ds(z + (r0 + 1), count), :],
        )
        return here - jnp.abs(u) * (here - across) - jnp.abs(v) * (here - along)

    out_copies = []
    for level in (1, 0):
        for j in range(-1, blocks + 1):
            block = first_block + j
            if j == -1:
                if first:
                    turned[0:MARGIN, :] = jnp.zeros((MARGIN, LANES), jnp.bfloat16)
                else:
                    turned[0:MARGIN, :] = turn(block, level)[LANES - MARGIN :, :]
            elif j == blocks:
                at = MARGIN + rows
                if final:
                    turned[at : at + MARGIN, :] = jnp.zeros((MARGIN, LANES), jnp.bfloat16)
                else:
                    turned[at : at + MARGIN, :] = turn(block, level)[:MARGIN, :]
            else:
                at = MARGIN + LANES * j
                turned[at : at + LANES, :] = turn(block, level)

        lhs = turned[...]
        for p in range(20 if level == 0 else 12):
            both = jnp.dot(lhs, spread[p], preferred_element_type=jnp.float32)
            coef[2 * p] = both[:, :LANES]
            coef[2 * p + 1] = both[:, LANES:]

        rims_at = MARGIN if first else 2 * MARGIN
        length = west.shape[2]

        def widen_rims(c, carry):
            for at, rim, before in (
                (c, west, None if first else west_before),
                (SUB + columns + c, east, None if first else east_before),
            ):
                if first:
                    even[at, 0:MARGIN, :] = jnp.zeros((MARGIN, LANES), jnp.float32)
                else:
                    end = before.shape[2]
                    even[at, 0 : 2 * MARGIN, :] = before[
                        level, c, end - 2 * MARGIN : end, :
                    ].astype(jnp.float32)
                even[at, rims_at : rims_at + length, :] = rim[level, c].astype(jnp.float32)
                if final:
                    even[at, span - MARGIN :, :] = jnp.zeros((MARGIN, LANES), jnp.float32)
            return carry

        def widen(c, carry):
            even[SUB + c, offset : offset + filled, :] = tracer[level, c, low:top, :].astype(
                jnp.float32
            )
            if first:
                even[SUB + c, 0:MARGIN, :] = jnp.zeros((MARGIN, LANES), jnp.float32)
            if final:
                even[SUB + c, span - MARGIN :, :] = jnp.zeros((MARGIN, LANES), jnp.float32)
            return carry

        lax.fori_loop(0, SUB, widen_rims, 0)
        lax.fori_loop(0, columns, widen, 0)

        def substep_one(c, carry):
            for r0, count in row_blocks(8, span - 16):
                odd[c, r0 : r0 + count, :] = step(even, c, c - 1, r0, count)
            return carry

        def substep_two(c, carry):
            for r0, count in row_blocks(8, span - 16):
                even[c, r0 : r0 + count, :] = step(odd, c, c - 1, r0, count)
            return carry

        lax.fori_loop(1, wide - 1, substep_one, 0)
        lax.fori_loop(2, wide - 2, substep_two, 0)

        for x in range(columns):
            c = x + SUB
            for r0, count in row_blocks(MARGIN, rows):
                tracer_now = step(even, c, c - 1, r0, count)
                if level == 0:
                    depth = coef[24 + x, r0 : r0 + count, :]
                    hot = jnp.where(coef[32 + x, r0 : r0 + count, :] == category, 1.0, 0.0)
                    speed = jnp.dot(
                        hot.astype(jnp.bfloat16), speeds[...], preferred_element_type=jnp.float32
                    )
                    tracer_now = tracer_now * depth / (depth + speed)
                result[level, x, r0 - MARGIN : r0 - MARGIN + count, :] = tracer_now
            rounded = result[level, x, :, :].astype(jnp.bfloat16)
            projected = lax.dot_general(
                table[...], rounded, (((1,), (1,)), ((), ())), preferred_element_type=jnp.float32
            )
            for b in range(blocks):
                block = first_block + b
                which = bins[x : x + 1, block * LANES : (block + 1) * LANES]
                dry = jnp.zeros((8, LANES), jnp.float32)
                wet = jnp.zeros((8, LANES), jnp.float32)
                for k in range(NBIN):
                    chosen = which == k
                    lanes = slice(b * LANES, (b + 1) * LANES)
                    dry = jnp.where(chosen, projected[8 * k : 8 * k + 8, lanes], dry)
                    wet = jnp.where(chosen, projected[64 + 8 * k : 72 + 8 * k, lanes], wet)
                moist = row(block, MOIST_ROW + 8 * level + x)
                depth_row = row(block, DEPTH_ROW + 8 * level + x)
                sun = row(block, SUN_ROW + x)
                growth = moist / (1.0 - moist)
                optical = (dry + growth * wet) * depth_row
                if level == 1:
                    thick[x, b] = optical
                    lit = weights * optical
                else:
                    overhead = pltpu.roll(thick[x, b], NW, 0)
                    lit = weights * optical * jnp.exp(-overhead / sun)
                at = 8 * level + x
                warm[b, at : at + 1, :] = sun * jnp.sum(lit, axis=0, keepdims=True)
        copy = pltpu.make_async_copy(
            result.at[level], out.at[level, :, start:stop, :], out_sems.at[level]
        )
        copy.start()
        out_copies.append(copy)

    copy = pltpu.make_async_copy(warm, heat.at[first_block : first_block + blocks], heat_sem.at[0])
    copy.start()
    out_copies.append(copy)
    for copy in out_copies:
        copy.wait()


def per_device(
    tracer_amounts,
    zonal_transit_ratio,
    meridional_transit_ratio,
    moisture_ratio,
    stratum_depths,
    sun_elevation_factor,
    thermal_anomaly,
    particle_class_map,
    ground_cover_kind,
    arid_extinction_table,
    swelling_factors,
    settling_velocities,
    arriving_irradiance,
):
    f32, bf16 = jnp.float32, jnp.bfloat16
    levels, columns, grid_rows, species = tracer_amounts.shape
    tile = thermal_anomaly.shape[1]
    gx, gy = lax.axis_size("gx"), lax.axis_size("gy")
    strips = ("gx", "gy")
    up = [(i, i + 1) for i in range(gx * gy - 1)]
    down = [(j, i) for i, j in up]
    gx_up = [(i, i + 1) for i in range(gx - 1)]
    gx_down = [(j, i) for i, j in gx_up]
    vmem = pl.BlockSpec(memory_space=pltpu.VMEM)
    smem = pl.BlockSpec(memory_space=pltpu.SMEM)
    hbm = pl.BlockSpec(memory_space=pltpu.HBM)

    bounds = [0]
    for rows in CHUNKS:
        bounds.append(bounds[-1] + rows)
    cuts = [0] + [b + MARGIN for b in bounds[1:-1]] + [grid_rows]
    wests, easts = [], []
    for low, top in zip(cuts[:-1], cuts[1:]):
        wests.append(lax.ppermute(tracer_amounts[:, columns - SUB :, low:top], strips, up))
        easts.append(lax.ppermute(tracer_amounts[:, :SUB, low:top], strips, down))

    def edge(pick, row):
        cut = [a[:, pick].reshape(-1, LANES) for a in (zonal_transit_ratio, meridional_transit_ratio)]
        return jnp.concatenate(cut + [thermal_anomaly[:, row]], axis=0)

    from_low = lax.ppermute(edge(slice(tile - RIM, tile), tile - 1), "gx", gx_up)
    from_high = lax.ppermute(edge(slice(0, RIM), 0), "gx", gx_down)

    mine = lax.axis_index("gy")
    place = mine.astype(jnp.int32).reshape(1)
    packed = pl.pallas_call(
        pack_kernel,
        out_shape=jax.ShapeDtypeStruct((gy, FIELD_ROWS, LANES), f32),
        in_specs=[smem] + [vmem] * 8,
        out_specs=vmem,
        scratch_shapes=[pltpu.VMEM((4, tile + 16, LANES), f32)],
        name="pack",
    )(
        place,
        zonal_transit_ratio,
        meridional_transit_ratio,
        moisture_ratio,
        stratum_depths,
        sun_elevation_factor,
        thermal_anomaly,
        from_low[: 4 * RIM],
        from_high[: 4 * RIM],
    )
    fields = lax.all_to_all(packed, "gy", split_axis=0, concat_axis=0, tiled=True)

    def rim_row(source):
        return lax.dynamic_slice(fields, (source, EDGE_ROW, 0), (1, 1, LANES)).reshape(1, LANES)

    warmed = pl.pallas_call(
        warm_kernel,
        out_shape=jax.ShapeDtypeStruct(thermal_anomaly.shape, f32),
        in_specs=[smem] + [vmem] * 5,
        out_specs=vmem,
        scratch_shapes=[pltpu.VMEM((tile + 16, LANES), f32)],
        name="warm",
    )(
        place,
        thermal_anomaly,
        from_low[4 * RIM :],
        from_high[4 * RIM :],
        rim_row(jnp.maximum(mine - 1, 0)),
        rim_row(jnp.minimum(mine + 1, gy - 1)),
    )

    spread = jnp.asarray(spread_matrix(), bf16)
    table = jnp.concatenate([arid_extinction_table, swelling_factors], axis=1).T
    parts, rest = [], settling_velocities
    for _ in range(3):
        part = lax.reduce_precision(rest, 8, 7)
        parts.append(part.astype(bf16))
        rest = rest - part
    parts.append(jnp.zeros((LANES - 3 * settling_velocities.shape[0], species), bf16))
    speeds = jnp.concatenate(parts, axis=0)
    zero = jnp.zeros((1,), jnp.int32)

    out = heat = None
    for k, rows in enumerate(CHUNKS):
        first, final = k == 0, k == len(CHUNKS) - 1
        span = rows + 2 * MARGIN
        operands = [
            zero,
            arriving_irradiance,
            fields,
            ground_cover_kind,
            particle_class_map,
            spread,
            table,
            speeds,
            tracer_amounts,
            wests[k],
            easts[k],
        ]
        specs = [smem, smem] + [vmem] * 9
        aliases = {}
        if not first:
            operands += [wests[k - 1], easts[k - 1], out, heat]
            specs += [vmem] * 2 + [hbm] * 2
            aliases = {13: 0, 14: 1}
        work = rows * columns * levels * species
        out, heat = pl.pallas_call(
            functools.partial(chunk_kernel, bounds[k], rows, grid_rows, first, final),
            out_shape=(
                jax.ShapeDtypeStruct(tracer_amounts.shape, f32),
                jax.ShapeDtypeStruct((gy, levels * columns, LANES), f32),
            ),
            in_specs=specs,
            out_specs=(hbm, hbm),
            scratch_shapes=[
                pltpu.VMEM((columns + 2 * SUB, span, LANES), f32),
                pltpu.VMEM((columns + 2 * SUB, span, LANES), f32),
                pltpu.VMEM((40, span, LANES), f32),
                pltpu.VMEM((span, LANES), bf16),
                pltpu.VMEM((levels, columns, rows, LANES), f32),
                pltpu.VMEM((columns, rows // LANES, 8, LANES), f32),
                pltpu.VMEM((rows // LANES, levels * columns, LANES), f32),
                pltpu.SemaphoreType.DMA((levels,)),
                pltpu.SemaphoreType.DMA((1,)),
            ],
            input_output_aliases=aliases,
            compiler_params=pltpu.CompilerParams(vmem_limit_bytes=40 * 1024 * 1024),
            cost_estimate=pl.CostEstimate(
                flops=60 * work, transcendentals=0, bytes_accessed=8 * work
            ),
        )(*operands)

    returned = lax.all_to_all(heat, "gy", split_axis=0, concat_axis=0, tiled=True)
    returned = returned.reshape(gy, levels, columns, LANES).transpose(1, 0, 2, 3)
    return out, warmed + returned.reshape(thermal_anomaly.shape)


def solution(mesh):
    return jax.shard_map(
        per_device,
        mesh=mesh,
        in_specs=(
            P(None, ("gx", "gy"), None, None),
            P(None, "gx", "gy"),
            P(None, "gx", "gy"),
            P(None, "gx", "gy"),
            P(None, "gx", "gy"),
            P("gx", "gy"),
            P(None, "gx", "gy"),
            P(("gx", "gy"), None),
            P(("gx", "gy"), None),
            P(),
            P(),
            P(),
            P(),
        ),
        out_specs=(P(None, ("gx", "gy"), None, None), P(None, "gx", "gy")),
        check_vma=False,
    )
```

profile of v0, /device:TPU:0, one launch (start us, length us, event | category | flops | bytes accessed | tf_op | source)
XLA Modules:
  0.0 127.5 jit_solution(7515288368736143546)
XLA Ops:
  0.7 2.5 %fusion.4 = (bf16[2,3,400,128]{3,2,1,0:T(8,128)(2,1)}, bf16[2,3,400,128]{3,2,1,0:T(8,128)(2,1)}) fusion(bf16[2,8,1024,128]{3,2,1,0:T(8,128)(2,1)} %refs_8_.7), kind=kLoop, calls=%fused_computation.15 | loop fusion | bytes 2457600 | tf_op jit(solution)/shard_map/slice | solution.py:326
  3.2 4.0 %collective-permute-start.8 = (bf16[2,3,400,128]{3,2,1,0:T(8,128)(2,1)}, bf16[2,3,400,128]{3,2,1,0:T(8,128)(2,1)S(1)}, u32[]{:S(2)}, u32[]{:S(2)}) collective-permute-start(bf16[2,3,400,128]{3,2,1,0:T(8,128)(2,1)} %get-tuple-element.19), channel_id=1, source_target_pairs={{0,1},{1,2},{2,3},{3,4},{4,5},{5,6},{6,7},{7,8},{8,9},{9,10},{10,1... | collective-permute-start | bytes 1843208 | tf_op jit(solution)/shard_map/ppermute | solution.py:325
  7.1 1.3 %collective-permute-start.9 = (bf16[2,3,400,128]{3,2,1,0:T(8,128)(2,1)}, bf16[2,3,400,128]{3,2,1,0:T(8,128)(2,1)S(1)}, u32[]{:S(2)}, u32[]{:S(2)}) collective-permute-start(bf16[2,3,400,128]{3,2,1,0:T(8,128)(2,1)} %get-tuple-element.18), channel_id=1, source_target_pairs={{1,0},{2,1},{3,2},{4,3},{5,4},{6,5},{7,6},{8,7},{9,8},{10,9},{11,1... | collective-permute-start | bytes 1843208 | tf_op jit(solution)/shard_map/ppermute | solution.py:326
  8.4 2.6 %fusion.5 = (bf16[2,3,256,128]{3,2,1,0:T(8,128)(2,1)}, bf16[2,3,256,128]{3,2,1,0:T(8,128)(2,1)}, bf16[2,3,256,128]{3,2,1,0:T(8,128)(2,1)}, bf16[2,3,256,128]{3,2,1,0:T(8,128)(2,1)}) fusion(bf16[2,8,1024,128]{3,2,1,0:T(8,128)(2,1)} %refs_8_.7), kind=kLoop, calls=%fused_computation.16 | loop fusion | bytes 3145728 | tf_op jit(solution)/shard_map/slice | solution.py:326
  11.0 4.6 %collective-permute-start.6 = (bf16[2,3,256,128]{3,2,1,0:T(8,128)(2,1)}, bf16[2,3,256,128]{3,2,1,0:T(8,128)(2,1)S(1)}, u32[]{:S(2)}, u32[]{:S(2)}) collective-permute-start(bf16[2,3,256,128]{3,2,1,0:T(8,128)(2,1)} %get-tuple-element.21), channel_id=1, source_target_pairs={{0,1},{1,2},{2,3},{3,4},{4,5},{5,6},{6,7},{7,8},{8,9},{9,10},{10,1... | collective-permute-start | bytes 1179656 | tf_op jit(solution)/shard_map/ppermute | solution.py:325
  17.7 2.2 %collective-permute-start = (f32[10,128]{1,0:T(8,128)S(1)}, f32[10,128]{1,0:T(8,128)S(1)}, u32[]{:S(2)}, u32[]{:S(2)}) collective-permute-start(f32[10,128]{1,0:T(8,128)S(1)} %pad_maximum_fusion), channel_id=1, source_target_pairs={{0,8},{8,16},{16,24},{24,32},{32,40},{40,48},{48,56},{56,64},{64,7... | collective-permute-start | bytes 15368 | tf_op jit(solution)/shard_map/ppermute | solution.py:332
  19.9 1.3 %collective-permute-start.1 = (f32[10,128]{1,0:T(8,128)S(1)}, f32[10,128]{1,0:T(8,128)S(1)}, u32[]{:S(2)}, u32[]{:S(2)}) collective-permute-start(f32[10,128]{1,0:T(8,128)S(1)} %pad_maximum_fusion.1), channel_id=1, source_target_pairs={{8,0},{16,8},{24,16},{32,24},{40,32},{48,40},{56,48},{64,56},{72,6... | collective-permute-start | bytes 15368 | tf_op jit(solution)/shard_map/ppermute | solution.py:333
  21.2 1.8 %fusion.6 = (bf16[2,3,112,128]{3,2,1,0:T(8,128)(2,1)}, bf16[2,3,112,128]{3,2,1,0:T(8,128)(2,1)}) fusion(bf16[2,8,1024,128]{3,2,1,0:T(8,128)(2,1)} %refs_8_.7), kind=kLoop, calls=%fused_computation.17 | loop fusion | bytes 688128 | tf_op jit(solution)/shard_map/slice | solution.py:326
  23.0 1.3 %collective-permute-start.7 = (bf16[2,3,256,128]{3,2,1,0:T(8,128)(2,1)}, bf16[2,3,256,128]{3,2,1,0:T(8,128)(2,1)}, u32[]{:S(2)}, u32[]{:S(2)}) collective-permute-start(bf16[2,3,256,128]{3,2,1,0:T(8,128)(2,1)} %get-tuple-element.20), channel_id=1, source_target_pairs={{1,0},{2,1},{3,2},{4,3},{5,4},{6,5},{7,6},{8,7},{9,8},{10,9},{11,1... | collective-permute-start | bytes 1179656 | tf_op jit(solution)/shard_map/ppermute | solution.py:326
  24.9 5.3 %collective-permute-start.4 = (bf16[2,3,256,128]{3,2,1,0:T(8,128)(2,1)}, bf16[2,3,256,128]{3,2,1,0:T(8,128)(2,1)}, u32[]{:S(2)}, u32[]{:S(2)}) collective-permute-start(bf16[2,3,256,128]{3,2,1,0:T(8,128)(2,1)} %get-tuple-element.23), channel_id=1, source_target_pairs={{0,1},{1,2},{2,3},{3,4},{4,5},{5,6},{6,7},{7,8},{8,9},{9,10},{10,1... | collective-permute-start | bytes 1179656 | tf_op jit(solution)/shard_map/ppermute | solution.py:325
  30.8 1.8 %pack.1 = f32[8,96,128]{2,1,0:T(8,128)} custom-call(s32[1]{0:T(128)} %bitcast.place, f32[2,64,128]{2,1,0:T(8,128)} %u.1, f32[2,64,128]{2,1,0:T(8,128)} %v.1, f32[2,64,128]{2,1,0:T(8,128)} %moisture.1, f32[2,64,128]{2,1,0:T(8,128)} %depth.1, f32[64,128]{1,0:T(8,128)} %sun.1, f32[2,64,128]{2,1,0:T(8,128)} %warmth.3, f32[8,128]{1,0:T(8,128)} %slice.72.low, ...), custom_call_target="tpu_custom_call" | custom-call | tf_op jit(solution)/shard_map/pack/pallas_call | solution.py:337
  32.6 8.1 %all-to-all-start = ((f32[8,96,128]{2,1,0:T(8,128)}), f32[8,96,128]{2,1,0:T(8,128)S(1)}, u32[]{:S(2)}, u32[]{:S(2)}) async-start(f32[8,96,128]{2,1,0:T(8,128)} %pack.1), calls=%async_computation | async-start | bytes 786432 | tf_op jit(solution)/shard_map/all_to_all | solution.py:355
  40.7 14.2 %collective-permute-done.6.refs_9_.refs_11_ = bf16[2,3,256,128]{3,2,1,0:T(8,128)(2,1)S(1)} collective-permute-done((bf16[2,3,256,128]{3,2,1,0:T(8,128)(2,1)}, bf16[2,3,256,128]{3,2,1,0:T(8,128)(2,1)S(1)}, u32[]{:S(2)}, u32[]{:S(2)}) %collective-permute-start.6) | collective-permute-done | bytes 393248 | tf_op jit(solution)/shard_map/ppermute | solution.py:325
  56.3 5.6 %collective-permute-start.2 = (bf16[2,3,112,128]{3,2,1,0:T(8,128)(2,1)}, bf16[2,3,112,128]{3,2,1,0:T(8,128)(2,1)}, u32[]{:S(2)}, u32[]{:S(2)}) collective-permute-start(bf16[2,3,112,128]{3,2,1,0:T(8,128)(2,1)} %get-tuple-element.25), channel_id=1, source_target_pairs={{0,1},{1,2},{2,3},{3,4},{4,5},{5,6},{6,7},{7,8},{8,9},{9,10},{10,1... | collective-permute-start | bytes 516104 | tf_op jit(solution)/shard_map/ppermute | solution.py:325
  64.4 12.1 %all-to-all-done.refs_2_ = f32[8,96,128]{2,1,0:T(8,128)S(1)} async-done(((f32[8,96,128]{2,1,0:T(8,128)}), f32[8,96,128]{2,1,0:T(8,128)S(1)}, u32[]{:S(2)}, u32[]{:S(2)}) %all-to-all-start) | async-done | bytes 393248 | tf_op jit(solution)/shard_map/all_to_all | solution.py:355
  76.5 2.2 %copy-done = bf16[2,8,1024,128]{3,2,1,0:T(8,128)(2,1)S(1)} copy-done((bf16[2,8,1024,128]{3,2,1,0:T(8,128)(2,1)S(1)}, bf16[2,8,1024,128]{3,2,1,0:T(8,128)(2,1)}, u32[]{:S(2)}) %copy-start) | copy-done | bytes 4194328
  78.7 11.1 %shard_map.149 = (f32[2,8,1024,128]{3,2,1,0:T(8,128)}, f32[8,16,128]{2,1,0:T(8,128)}) custom-call(s32[1]{0:T(128)} %constant.4.clone.1.refs_0_, f32[4]{0:T(128)S(1)} %copy-done.4, f32[8,96,128]{2,1,0:T(8,128)S(1)} %all-to-all-done.refs_2_, s32[8,1024]{1,0:T(8,128)S(1)} %copy-done.2, s32[8,1024]{1,0:T(8,128)S(1)} %copy-done.3, ...), custom_call_target="tpu_custom_call" | custom-call | flops 47185920 | bytes 6291456 | tf_op jit(solution)/shard_map/pallas_call | solution.py:411
  89.9 8.8 %shard_map.150 = (f32[2,8,1024,128]{3,2,1,0:T(8,128)}, f32[8,16,128]{2,1,0:T(8,128)}) custom-call(s32[1]{0:T(128)} %constant.4.clone.1.refs_0_, f32[4]{0:T(128)S(1)} %copy-done.4, f32[8,96,128]{2,1,0:T(8,128)S(1)} %all-to-all-done.refs_2_, s32[8,1024]{1,0:T(8,128)S(1)} %copy-done.2, ...), custom_call_target="tpu_custom_call", output_to_operand_aliasing={{0}: (13, {}), {1}: (14, {})} | custom-call | flops 31457280 | bytes 4194304 | tf_op jit(solution)/shard_map/pallas_call | solution.py:411
  98.7 9.1 %shard_map.151 = (f32[2,8,1024,128]{3,2,1,0:T(8,128)}, f32[8,16,128]{2,1,0:T(8,128)}) custom-call(s32[1]{0:T(128)} %constant.4.clone.1.refs_0_, f32[4]{0:T(128)S(1)} %copy-done.4, f32[8,96,128]{2,1,0:T(8,128)S(1)} %all-to-all-done.refs_2_, s32[8,1024]{1,0:T(8,128)S(1)} %copy-done.2, ...), custom_call_target="tpu_custom_call", output_to_operand_aliasing={{0}: (13, {}), {1}: (14, {})} | custom-call | flops 31457280 | bytes 4194304 | tf_op jit(solution)/shard_map/pallas_call | solution.py:411
  107.8 5.8 %shard_map.152 = (f32[2,8,1024,128]{3,2,1,0:T(8,128)}, f32[8,16,128]{2,1,0:T(8,128)}) custom-call(s32[1]{0:T(128)} %constant.4.clone.1.refs_0_, f32[4]{0:T(128)S(1)} %copy-done.4, f32[8,96,128]{2,1,0:T(8,128)S(1)} %all-to-all-done.refs_2_, s32[8,1024]{1,0:T(8,128)S(1)} %copy-done.2, ...), custom_call_target="tpu_custom_call", output_to_operand_aliasing={{0}: (13, {}), {1}: (14, {})} | custom-call | flops 15728640 | bytes 2097152 | tf_op jit(solution)/shard_map/pallas_call | solution.py:411
  113.6 6.1 %all-to-all-start.1 = ((f32[8,16,128]{2,1,0:T(8,128)}), f32[8,16,128]{2,1,0:T(8,128)S(1)}, u32[]{:S(2)}, u32[]{:S(2)}) async-start(f32[8,16,128]{2,1,0:T(8,128)} %get-tuple-element.17), calls=%async_computation.1 | async-start | bytes 131072 | tf_op jit(solution)/shard_map/all_to_all | solution.py:437
  120.3 1.7 %warm.1 = f32[2,64,128]{2,1,0:T(8,128)} custom-call(s32[1]{0:T(128)} %bitcast.place, f32[2,64,128]{2,1,0:T(8,128)} %warmth.3, f32[2,128]{1,0:T(2,128)} %slice.74.low, f32[2,128]{1,0:T(2,128)} %slice.75.high, f32[1,128]{1,0:T(1,128)} %get-tuple-element.27.left, f32[1,128]{1,0:T(1,128)} %get-tuple-element.26.right), custom_call_target="tpu_custom_call" | custom-call | tf_op jit(solution)/shard_map/warm/pallas_call | solution.py:360
  122.1 4.0 %all-to-all-done.1 = f32[8,16,128]{2,1,0:T(8,128)S(1)} async-done(((f32[8,16,128]{2,1,0:T(8,128)}), f32[8,16,128]{2,1,0:T(8,128)S(1)}, u32[]{:S(2)}, u32[]{:S(2)}) %all-to-all-start.1) | async-done | bytes 65568 | tf_op jit(solution)/shard_map/all_to_all | solution.py:437
  126.0 1.5 %bitcast_add_fusion = f32[2,64,128]{2,1,0:T(8,128)} fusion(f32[2,64,128]{2,1,0:T(8,128)} %warm.1, f32[8,16,128]{2,1,0:T(8,128)S(1)} %all-to-all-done.1), kind=kLoop, calls=%fused_computation | loop fusion | flops 16384 | bytes 196608 | tf_op jit(solution)/shard_map/add | solution.py:439
  (41 shorter events, 7.9 us)
Async XLA Ops:
  0.6 75.9 %copy-start.1 = (bf16[20,128,256]{2,1,0:T(8,128)(2,1)S(1)}, bf16[20,128,256]{2,1,0:T(8,128)(2,1)}, u32[]{:S(2)}) copy-start(bf16[20,128,256]{2,1,0:T(8,128)(2,1)} %constant.23.clone.refs_5_) | copy-start | bytes 3932164
  0.6 55.5 %copy-start.7 = (f32[24,128]{1,0:T(8,128)S(1)}, f32[24,128]{1,0:T(8,128)}, u32[]{:S(2)}) copy-start(f32[24,128]{1,0:T(8,128)} %param.25) | copy-start | bytes 36868
  0.7 62.6 %copy-start.6 = (bf16[128,64]{0,1:T(8,128)(2,1)S(1)}, bf16[128,64]{0,1:T(8,128)(2,1)}, u32[]{:S(2)}) copy-start(bf16[128,64]{0,1:T(8,128)(2,1)} %param.23) | copy-start | bytes 49156
  0.7 62.6 %copy-start.5 = (bf16[128,64]{0,1:T(8,128)(2,1)S(1)}, bf16[128,64]{0,1:T(8,128)(2,1)}, u32[]{:S(2)}) copy-start(bf16[128,64]{0,1:T(8,128)(2,1)} %param.24) | copy-start | bytes 49156
  0.7 75.8 %copy-start.3 = (s32[8,1024]{1,0:T(8,128)S(1)}, s32[8,1024]{1,0:T(8,128)}, u32[]{:S(2)}) copy-start(s32[8,1024]{1,0:T(8,128)} %refs_4_.7) | copy-start | bytes 98308
  0.7 75.8 %copy-start.2 = (s32[8,1024]{1,0:T(8,128)S(1)}, s32[8,1024]{1,0:T(8,128)}, u32[]{:S(2)}) copy-start(s32[8,1024]{1,0:T(8,128)} %refs_3_.7) | copy-start | bytes 98308
  0.7 75.8 %copy-start.4 = (f32[4]{0:T(128)S(1)}, f32[4]{0:T(128)}, u32[]{:S(2)}) copy-start(f32[4]{0:T(128)} %refs_1_.7) | copy-start | bytes 52
  3.2 53.1 %collective-permute-start.8 = (bf16[2,3,400,128]{3,2,1,0:T(8,128)(2,1)}, bf16[2,3,400,128]{3,2,1,0:T(8,128)(2,1)S(1)}, u32[]{:S(2)}, u32[]{:S(2)}) collective-permute-start(bf16[2,3,400,128]{3,2,1,0:T(8,128)(2,1)} %get-tuple-element.19), channel_id=1, source_target_pairs={{0,1},{1,2},{2,3},{3,4},{4,5},{5,6},{6,7},{7,8},{8,9},{9,10},{10,1... | collective-permute-start | bytes 1843208 | tf_op jit(solution)/shard_map/ppermute | solution.py:325
  7.1 54.7 %collective-permute-start.9 = (bf16[2,3,400,128]{3,2,1,0:T(8,128)(2,1)}, bf16[2,3,400,128]{3,2,1,0:T(8,128)(2,1)S(1)}, u32[]{:S(2)}, u32[]{:S(2)}) collective-permute-start(bf16[2,3,400,128]{3,2,1,0:T(8,128)(2,1)} %get-tuple-element.18), channel_id=1, source_target_pairs={{1,0},{2,1},{3,2},{4,3},{5,4},{6,5},{7,6},{8,7},{9,8},{10,9},{11,1... | collective-permute-start | bytes 1843208 | tf_op jit(solution)/shard_map/ppermute | solution.py:326
  11.0 43.9 %collective-permute-start.6 = (bf16[2,3,256,128]{3,2,1,0:T(8,128)(2,1)}, bf16[2,3,256,128]{3,2,1,0:T(8,128)(2,1)S(1)}, u32[]{:S(2)}, u32[]{:S(2)}) collective-permute-start(bf16[2,3,256,128]{3,2,1,0:T(8,128)(2,1)} %get-tuple-element.21), channel_id=1, source_target_pairs={{0,1},{1,2},{2,3},{3,4},{4,5},{5,6},{6,7},{7,8},{8,9},{9,10},{10,1... | collective-permute-start | bytes 1179656 | tf_op jit(solution)/shard_map/ppermute | solution.py:325
  17.7 5.2 %collective-permute-start = (f32[10,128]{1,0:T(8,128)S(1)}, f32[10,128]{1,0:T(8,128)S(1)}, u32[]{:S(2)}, u32[]{:S(2)}) collective-permute-start(f32[10,128]{1,0:T(8,128)S(1)} %pad_maximum_fusion), channel_id=1, source_target_pairs={{0,8},{8,16},{16,24},{24,32},{32,40},{40,48},{48,56},{56,64},{64,7... | collective-permute-start | bytes 15368 | tf_op jit(solution)/shard_map/ppermute | solution.py:332
  19.9 5.0 %collective-permute-start.1 = (f32[10,128]{1,0:T(8,128)S(1)}, f32[10,128]{1,0:T(8,128)S(1)}, u32[]{:S(2)}, u32[]{:S(2)}) collective-permute-start(f32[10,128]{1,0:T(8,128)S(1)} %pad_maximum_fusion.1), channel_id=1, source_target_pairs={{8,0},{16,8},{24,16},{32,24},{40,32},{48,40},{56,48},{64,56},{72,6... | collective-permute-start | bytes 15368 | tf_op jit(solution)/shard_map/ppermute | solution.py:333
  23.0 66.9 %collective-permute-start.7 = (bf16[2,3,256,128]{3,2,1,0:T(8,128)(2,1)}, bf16[2,3,256,128]{3,2,1,0:T(8,128)(2,1)}, u32[]{:S(2)}, u32[]{:S(2)}) collective-permute-start(bf16[2,3,256,128]{3,2,1,0:T(8,128)(2,1)} %get-tuple-element.20), channel_id=1, source_target_pairs={{1,0},{2,1},{3,2},{4,3},{5,4},{6,5},{7,6},{8,7},{9,8},{10,9},{11,1... | collective-permute-start | bytes 1179656 | tf_op jit(solution)/shard_map/ppermute | solution.py:326
  24.9 73.8 %collective-permute-start.4 = (bf16[2,3,256,128]{3,2,1,0:T(8,128)(2,1)}, bf16[2,3,256,128]{3,2,1,0:T(8,128)(2,1)}, u32[]{:S(2)}, u32[]{:S(2)}) collective-permute-start(bf16[2,3,256,128]{3,2,1,0:T(8,128)(2,1)} %get-tuple-element.23), channel_id=1, source_target_pairs={{0,1},{1,2},{2,3},{3,4},{4,5},{5,6},{6,7},{7,8},{8,9},{9,10},{10,1... | collective-permute-start | bytes 1179656 | tf_op jit(solution)/shard_map/ppermute | solution.py:325
  32.6 43.9 %all-to-all-start = ((f32[8,96,128]{2,1,0:T(8,128)}), f32[8,96,128]{2,1,0:T(8,128)S(1)}, u32[]{:S(2)}, u32[]{:S(2)}) async-start(f32[8,96,128]{2,1,0:T(8,128)} %pack.1), calls=%async_computation | async-start | bytes 786432 | tf_op jit(solution)/shard_map/all_to_all | solution.py:355
  54.9 43.8 %collective-permute-start.5 = (bf16[2,3,256,128]{3,2,1,0:T(8,128)(2,1)}, bf16[2,3,256,128]{3,2,1,0:T(8,128)(2,1)}, u32[]{:S(2)}, u32[]{:S(2)}) collective-permute-start(bf16[2,3,256,128]{3,2,1,0:T(8,128)(2,1)} %get-tuple-element.22), channel_id=1, source_target_pairs={{1,0},{2,1},{3,2},{4,3},{5,4},{6,5},{7,6},{8,7},{9,8},{10,9},{11,1... | collective-permute-start | bytes 1179656 | tf_op jit(solution)/shard_map/ppermute | solution.py:326
  56.3 51.5 %collective-permute-start.2 = (bf16[2,3,112,128]{3,2,1,0:T(8,128)(2,1)}, bf16[2,3,112,128]{3,2,1,0:T(8,128)(2,1)}, u32[]{:S(2)}, u32[]{:S(2)}) collective-permute-start(bf16[2,3,112,128]{3,2,1,0:T(8,128)(2,1)} %get-tuple-element.25), channel_id=1, source_target_pairs={{0,1},{1,2},{2,3},{3,4},{4,5},{5,6},{6,7},{7,8},{8,9},{9,10},{10,1... | collective-permute-start | bytes 516104 | tf_op jit(solution)/shard_map/ppermute | solution.py:325
  61.9 46.0 %collective-permute-start.3 = (bf16[2,3,112,128]{3,2,1,0:T(8,128)(2,1)}, bf16[2,3,112,128]{3,2,1,0:T(8,128)(2,1)}, u32[]{:S(2)}, u32[]{:S(2)}) collective-permute-start(bf16[2,3,112,128]{3,2,1,0:T(8,128)(2,1)} %get-tuple-element.24), channel_id=1, source_target_pairs={{1,0},{2,1},{3,2},{4,3},{5,4},{6,5},{7,6},{8,7},{9,8},{10,9},{11,1... | collective-permute-start | bytes 516104 | tf_op jit(solution)/shard_map/ppermute | solution.py:326
  76.5 2.2 %copy-start = (bf16[2,8,1024,128]{3,2,1,0:T(8,128)(2,1)S(1)}, bf16[2,8,1024,128]{3,2,1,0:T(8,128)(2,1)}, u32[]{:S(2)}) copy-start(bf16[2,8,1024,128]{3,2,1,0:T(8,128)(2,1)} %refs_8_.7) | copy-start | bytes 12582916
  113.6 12.4 %all-to-all-start.1 = ((f32[8,16,128]{2,1,0:T(8,128)}), f32[8,16,128]{2,1,0:T(8,128)S(1)}, u32[]{:S(2)}, u32[]{:S(2)}) async-start(f32[8,16,128]{2,1,0:T(8,128)} %get-tuple-element.17), calls=%async_computation.1 | async-start | bytes 131072 | tf_op jit(solution)/shard_map/all_to_all | solution.py:437
where the time goes:
time: 128 us
  starting transfers between devices  42.2 us (33%)
  Pallas kernels  38.4 us (30%)
  waiting for transfers between devices  30.3 us (24%)
  local copies, waits for them, and re-layouts  14.1 us (11%)
  other arithmetic  1.59 us (1%)
    pallas_call x4, Pallas kernels, per_device(): pl.pallas_call(functools.partial(chunk_kernel, bounds[k], rows, grid_rows...  34.9 us
    ppermute x4, starting transfers between devices, per_device(): lax.ppermute(tracer_amounts[:, columns - SUB:, low:top], strips, up)  19.4 us
    ppermute x4, waiting for transfers between devices, per_device(): lax.ppermute(tracer_amounts[:, columns - SUB:, low:top], strips, up)  14.2 us
    all_to_all x1, waiting for transfers between devices, per_device(): lax.all_to_all(packed, 'gy', split_axis=0, concat_axis=0, tiled=True)  12.1 us
    all_to_all x1, starting transfers between devices, per_device(): lax.all_to_all(packed, 'gy', split_axis=0, concat_axis=0, tiled=True)  8.13 us
    slice x3, local copies, waits for them, and re-layouts, per_device(): easts.append(lax.ppermute(tracer_amounts[:, :SUB, low:top], strips, down))  6.79 us
    all_to_all x1, starting transfers between devices, per_device(): lax.all_to_all(heat, 'gy', split_axis=0, concat_axis=0, tiled=True)  6.13 us
    ppermute x4, starting transfers between devices, per_device(): easts.append(lax.ppermute(tracer_amounts[:, :SUB, low:top], strips, down))  5.13 us
  transfers between devices with their start and end apart: 12, of which 3 were waited for; matrix products, arithmetic and copies ran while one was open for 8% of the time, Pallas kernels for 26%

commit v1 on v0

v1 whole, which is shorter than its diff:
```python
import functools

import jax
import jax.numpy as jnp
import numpy as np
from jax import lax
from jax.experimental import pallas as pl
from jax.experimental.pallas import tpu as pltpu
from jax.sharding import PartitionSpec as P


SUB = 3
NBIN = 8
NW = 4
SPREAD_FACTOR = 0.2

LANES = 128
MARGIN = 16
NEAR = 8
RIM = 2
CHUNKS = (2, 3, 2, 1)

UV_ROWS = 24
MOIST_ROW = 48
DEPTH_ROW = 64
SUN_ROW = 80
EDGE_ROW = 88
FIELD_ROWS = 96
PAIRS = 20


def spread_matrix():
    out = np.zeros((PAIRS, LANES, 2 * LANES), np.float32)
    for p in range(12):
        for part in range(3):
            out[p, 24 * part + p, :LANES] = 1.0
            out[p, 24 * part + 12 + p, LANES:] = 1.0
    for x in range(8):
        for part in range(3):
            out[12 + x, 72 + 8 * part + x, :LANES] = 1.0
        out[12 + x, 96 + x, LANES:] = 1.0
    return out


def three_parts(x):
    high = x.astype(jnp.bfloat16).astype(jnp.float32)
    rest = x - high
    middle = rest.astype(jnp.bfloat16).astype(jnp.float32)
    return [high, middle, rest - middle]


def chunk_rows(k):
    start = sum(CHUNKS[:k]) * LANES
    stop = start + CHUNKS[k] * LANES
    low = start - MARGIN if k == 0 else start + MARGIN
    return low, stop + (0 if k == len(CHUNKS) - 1 else MARGIN)


def slice_pieces(low, top):
    cuts = [low] + [c for c in range(-LANES, top, LANES) if low < c < top] + [top]
    return list(zip(cuts[:-1], cuts[1:]))


def slice_copies(chunks, place, tracer, outs, sems):
    mine = place[0]
    blocks = tracer.shape[2] // LANES
    columns = tracer.shape[1]
    copies = []
    for n, k in enumerate(chunks):
        low, top = chunk_rows(k)
        for side in range(2):
            target = lax.rem(mine + (1 if side == 0 else blocks - 1), blocks)
            first = columns - SUB if side == 0 else 0
            for a, b in slice_pieces(low, top):
                block = lax.rem(target + 1 + (a // LANES) + blocks, blocks)
                row = pl.multiple_of(block * LANES + a % LANES, MARGIN)
                copies.append(
                    pltpu.make_async_copy(
                        tracer.at[:, first : first + SUB, pl.ds(row, b - a), :],
                        outs[2 * n + side].at[:, :, a - low : b - low, :],
                        sems.at[len(copies)],
                    )
                )
    return copies


def copy_count(chunks):
    return sum(2 * len(slice_pieces(*chunk_rows(k))) for k in chunks)


def first_slice_kernel(place, tracer, u, v, warmth, up, down, rim_up, rim_down, sems):
    copies = slice_copies((0,), place, tracer, (up, down), sems)
    for copy in copies:
        copy.start()
    span = u.shape[1]
    for f in range(4):
        source = (u, v)[f // 2]
        rim_up[RIM * f : RIM * (f + 1), :] = source[f % 2, span - RIM : span, :]
        rim_down[RIM * f : RIM * (f + 1), :] = source[f % 2, 0:RIM, :]
    for level in range(2):
        at = 4 * RIM + level
        rim_up[at : at + 1, :] = warmth[level, span - 1 : span, :]
        rim_down[at : at + 1, :] = warmth[level, 0:1, :]
    at = 4 * RIM + 2
    rim_up[at:, :] = jnp.zeros((rim_up.shape[0] - at, LANES), jnp.float32)
    rim_down[at:, :] = jnp.zeros((rim_up.shape[0] - at, LANES), jnp.float32)
    for copy in copies:
        copy.wait()


def later_slice_kernel(place, tracer, *refs):
    outs, sems = refs[:-1], refs[-1]
    copies = slice_copies(tuple(range(1, len(CHUNKS))), place, tracer, outs, sems)
    for copy in copies:
        copy.start()
    for copy in copies:
        copy.wait()


def pack_kernel(place, u, v, moisture, depth, sun, warmth, low, high, out, ext):
    mine = place[0]
    parts = u.shape[1] // 8
    for f in range(4):
        source = (u, v)[f // 2]
        ext[f, 8 : 8 + u.shape[1], :] = source[f % 2]
        ext[f, 8 - RIM : 8, :] = low[RIM * f : RIM * (f + 1), :]
        ext[f, 8 + u.shape[1] : 8 + u.shape[1] + RIM, :] = high[RIM * f : RIM * (f + 1), :]
    turned = warmth[...].reshape(2 * u.shape[1], LANES).T
    last = turned[LANES - 1 :, :]
    initial = turned[:1, :]
    wide = 8 + 2 * RIM
    for d in range(parts):
        for level in range(2):
            base = UV_ROWS * level
            out[d, base : base + wide, :] = ext[level, 8 * d + 8 - RIM : 8 * d + 16 + RIM, :]
            out[d, base + wide : base + 2 * wide, :] = ext[
                2 + level, 8 * d + 8 - RIM : 8 * d + 16 + RIM, :
            ]
            out[d, MOIST_ROW + 8 * level : MOIST_ROW + 8 * level + 8, :] = moisture[
                level, 8 * d : 8 * d + 8, :
            ]
            out[d, DEPTH_ROW + 8 * level : DEPTH_ROW + 8 * level + 8, :] = depth[
                level, 8 * d : 8 * d + 8, :
            ]
        out[d, SUN_ROW : SUN_ROW + 8, :] = sun[8 * d : 8 * d + 8, :]
        row = jnp.where(mine + 1 == d, last, jnp.where(mine - 1 == d, initial, 0.0))
        out[d, EDGE_ROW : EDGE_ROW + 8, :] = jnp.broadcast_to(row, (8, LANES))


def turn_kernel(fields, kind, bins, turned, classes):
    for block in range(fields.shape[0]):
        lanes = slice(block * LANES, (block + 1) * LANES)
        classes[block] = bins[:, lanes]
        for level in range(2):
            parts = three_parts(fields[block, UV_ROWS * level : UV_ROWS * (level + 1), :])
            if level == 0:
                parts += three_parts(fields[block, DEPTH_ROW : DEPTH_ROW + 8, :])
                parts.append(kind[:, lanes].astype(jnp.float32))
                parts.append(jnp.zeros((24, LANES), jnp.float32))
            else:
                parts.append(jnp.zeros((56, LANES), jnp.float32))
            turned[level, block] = jnp.concatenate(parts, axis=0).T.astype(jnp.bfloat16)


def warm_kernel(place, warmth, low, high, fields, out, ext):
    mine = place[0]
    tiles = fields.shape[0]
    span = warmth.shape[1]
    lane = lax.broadcasted_iota(jnp.int32, (span, LANES), 1)
    left = fields[jnp.maximum(mine - 1, 0), EDGE_ROW : EDGE_ROW + 1, :]
    right = fields[jnp.minimum(mine + 1, tiles - 1), EDGE_ROW : EDGE_ROW + 1, :]
    at = 4 * RIM
    for level in range(2):
        here = warmth[level]
        ext[8 : 8 + span, :] = here
        ext[7:8, :] = low[at + level : at + level + 1, :]
        ext[8 + span : 9 + span, :] = high[at + level : at + level + 1, :]
        left_rows = jnp.broadcast_to(left[:, level * span : (level + 1) * span], (LANES, span)).T
        right_rows = jnp.broadcast_to(right[:, level * span : (level + 1) * span], (LANES, span)).T
        west = jnp.where(lane == 0, left_rows, pltpu.roll(here, 1, 1))
        east = jnp.where(lane == LANES - 1, right_rows, pltpu.roll(here, LANES - 1, 1))
        laplace = ext[9 : 9 + span, :] + ext[7 : 7 + span, :] + east + west - 4.0 * here
        out[level] = here + SPREAD_FACTOR * laplace


def row_blocks(first, count, size):
    return [(r, min(size, first + count - r)) for r in range(first, first + count, size)]


def chunk_kernel(k, *refs):
    first, final = k == 0, k == len(CHUNKS) - 1
    count = CHUNKS[k]
    refs = list(refs)
    place, sunlight, fields, classes, turned, spread, table, speeds, tracer = refs[:9]
    del refs[:9]
    west, east = refs[:2]
    del refs[:2]
    before = (None, None)
    if not first:
        before = refs[:2]
        del refs[:2]
        around = (None, None)
        if final:
            around = refs[:2]
            del refs[:2]
            del refs[:1]
        else:
            del refs[:2]
    out, heat = refs[:2]
    even, odd, coef, result, thick, warm, out_sems, heat_sems = refs[2:]

    columns = 8
    wide = columns + 2 * SUB
    mine, z = place[0], place[1]
    blocks = fields.shape[0]
    grid_rows = tracer.shape[2]
    top = MARGIN + LANES

    sublane = lax.broadcasted_iota(jnp.int32, (8, LANES), 0)
    weights = jnp.zeros((8, LANES), jnp.float32)
    for w in range(NW):
        weights = jnp.where(sublane == NW + w, sunlight[w], weights)
    lane = lax.broadcasted_iota(jnp.int32, (1, LANES), 1)
    category = jnp.where(lane < 72, lane % 24, -1).astype(jnp.float32)

    def wide_of(x):
        return x.astype(jnp.float32)

    def copies(j, slot, which=None):
        block = lax.rem(mine + 1 + sum(CHUNKS[:k]) + j, blocks)
        row = pl.multiple_of(block * LANES, LANES)
        these = []
        for level in (0, 1) if which is None else (which,):
            if level < 2:
                source, target = result.at[slot, level], out.at[level, :, pl.ds(row, LANES), :]
                these.append(pltpu.make_async_copy(source, target, out_sems.at[slot, level]))
        if which == 2 or (which is None and not final):
            these.append(pltpu.make_async_copy(warm.at[slot], heat.at[block], heat_sems.at[slot]))
        return these

    def step(source, c, i, r0, n):
        here = source[c, r0 : r0 + n, :]
        u = coef[2 * i, r0 - NEAR : r0 - NEAR + n, :]
        v = coef[2 * i + 1, r0 - NEAR : r0 - NEAR + n, :]
        across = jnp.where(u > 0.0, source[c - 1, r0 : r0 + n, :], source[c + 1, r0 : r0 + n, :])
        along = jnp.where(
            v > 0.0, source[c, pl.ds(z + (r0 - 1), n), :], source[c, pl.ds(z + (r0 + 1), n), :]
        )
        return here - jnp.abs(u) * (here - across) - jnp.abs(v) * (here - along)

    def one_block(j, carry):
        slot = lax.rem(j, 2)
        block = lax.rem(mine + 1 + sum(CHUNKS[:k]) + j, blocks)
        row = pl.multiple_of(block * LANES, LANES)
        low_row = pl.multiple_of(jnp.maximum(row - MARGIN, 0), MARGIN)
        high_row = pl.multiple_of(jnp.minimum(row + LANES, grid_rows - MARGIN), MARGIN)
        low_block = jnp.maximum(block - 1, 0)
        high_block = jnp.minimum(block + 1, blocks - 1)
        has_low = jnp.where(block != 0, 1.0, 0.0)
        has_high = jnp.where(block != blocks - 1, 1.0, 0.0)

        if count > 2:

            @pl.when(j >= 2)
            def _():
                for copy in copies(j - 2, slot):
                    copy.wait()

        for level in (1, 0):
            low_margin = wide_of(turned[level, low_block, LANES - MARGIN :, :]) * has_low
            high_margin = wide_of(turned[level, high_block, :MARGIN, :]) * has_high
            middle = turned[level, block]
            lhs = jnp.concatenate(
                [low_margin.astype(jnp.bfloat16), middle, high_margin.astype(jnp.bfloat16)], axis=0
            )

            def widen(at, low, head, tail, high):
                even[at, NEAR:MARGIN, :] = wide_of(low)[NEAR:, :] * has_low
                even[at, MARGIN : 2 * MARGIN, :] = wide_of(head)
                even[at, 2 * MARGIN : top, :] = wide_of(tail)
                even[at, top : top + NEAR, :] = wide_of(high)[:NEAR, :] * has_high

            for x in range(columns):
                widen(
                    SUB + x,
                    tracer[level, x, pl.ds(low_row, MARGIN), :],
                    tracer[level, x, pl.ds(row, MARGIN), :],
                    tracer[level, x, pl.ds(pl.multiple_of(row + MARGIN, MARGIN), LANES - MARGIN), :],
                    tracer[level, x, pl.ds(high_row, MARGIN), :],
                )

            def rims(at_start):
                for side, (rim, prior) in enumerate(zip((west, east), before)):
                    for c in range(SUB):
                        at = c + side * (SUB + columns)
                        if at_start:
                            end = prior.shape[2]
                            low = prior[level, c, end - 2 * MARGIN : end - MARGIN, :]
                            head = prior[level, c, end - MARGIN : end, :]
                            tail = rim[level, c, 0 : LANES - MARGIN, :]
                            if final:
                                high = around[side][level, c, MARGIN : 2 * MARGIN, :]
                            else:
                                high = rim[level, c, LANES - MARGIN : LANES, :]
                        else:
                            base = j * LANES + (0 if first else -2 * MARGIN)
                            low, head, tail, high = (
                                rim[level, c, pl.ds(pl.multiple_of(base + a, MARGIN), n), :]
                                for a, n in (
                                    (0, MARGIN),
                                    (MARGIN, MARGIN),
                                    (2 * MARGIN, LANES - MARGIN),
                                    (top, MARGIN),
                                )
                            )
                        widen(at, low, head, tail, high)

            if first:
                rims(False)
            elif count == 1:
                rims(True)
            else:
                pl.when(j == 0)(functools.partial(rims, True))
                pl.when(j != 0)(functools.partial(rims, False))

            for c in range(1, wide - 1):
                both = jnp.dot(lhs, spread[c - 1], preferred_element_type=jnp.float32)
                coef[2 * c - 2] = both[NEAR : top + NEAR, :LANES]
                coef[2 * c - 1] = both[NEAR : top + NEAR, LANES:]
                for r0, n in row_blocks(NEAR, LANES + 2 * NEAR, 72):
                    odd[c, r0 : r0 + n, :] = step(even, c, c - 1, r0, n)
            for c in range(2, wide - 2):
                for r0, n in row_blocks(NEAR, LANES + 2 * NEAR, 72):
                    even[c, r0 : r0 + n, :] = step(odd, c, c - 1, r0, n)

            for x in range(columns):
                c = x + SUB
                if level == 0:
                    pair = jnp.dot(middle, spread[12 + x], preferred_element_type=jnp.float32)
                    depth = pair[:, :LANES]
                    hot = jnp.where(pair[:, LANES:] == category, 1.0, 0.0).astype(jnp.bfloat16)
                    speed = jnp.dot(hot, speeds[...], preferred_element_type=jnp.float32)
                for r0, n in row_blocks(MARGIN, LANES, 64):
                    now = step(even, c, c - 1, r0, n)
                    if level == 0:
                        part = slice(r0 - MARGIN, r0 - MARGIN + n)
                        now = now * depth[part] / (depth[part] + speed[part])
                    result[slot, level, x, r0 - MARGIN : r0 - MARGIN + n, :] = now
                rounded = result[slot, level, x].astype(jnp.bfloat16)
                projected = lax.dot_general(
                    table[...], rounded, (((1,), (1,)), ((), ())), preferred_element_type=jnp.float32
                )
                which = classes[block, x : x + 1, :]
                dry = jnp.zeros((8, LANES), jnp.float32)
                wet = jnp.zeros((8, LANES), jnp.float32)
                for b in range(NBIN):
                    dry = jnp.where(which == b, projected[8 * b : 8 * b + 8], dry)
                    wet = jnp.where(which == b, projected[64 + 8 * b : 72 + 8 * b], wet)
                at = 8 * level + x
                moist = fields[block, MOIST_ROW + at : MOIST_ROW + at + 1, :]
                thickness = fields[block, DEPTH_ROW + at : DEPTH_ROW + at + 1, :]
                sun = fields[block, SUN_ROW + x : SUN_ROW + x + 1, :]
                growth = moist / (1.0 - moist)
                optical = (dry + growth * wet) * thickness
                if level == 1:
                    thick[x] = optical
                    lit = weights * optical
                else:
                    overhead = pltpu.roll(thick[x], NW, 0)
                    lit = weights * optical * jnp.exp(-overhead / sun)
                lit = sun * jnp.sum(lit, axis=0, keepdims=True)
                if final:
                    heat[at : at + 1, :] = lit
                else:
                    warm[slot, at : at + 1, :] = lit
            copies(j, slot, level)[0].start()
        if not final:
            copies(j, slot, 2)[0].start()
        return carry

    if count == 1:
        one_block(0, 0)
    else:
        lax.fori_loop(0, count, one_block, 0)
    for j in range(max(count - 2, 0), count):
        for copy in copies(j, j % 2):
            copy.wait()
    if first:
        copy = pltpu.make_async_copy(warm.at[0], heat.at[mine], heat_sems.at[0])
        copy.start()
        copy.wait()


def per_device(
    tracer_amounts,
    zonal_transit_ratio,
    meridional_transit_ratio,
    moisture_ratio,
    stratum_depths,
    sun_elevation_factor,
    thermal_anomaly,
    particle_class_map,
    ground_cover_kind,
    arid_extinction_table,
    swelling_factors,
    settling_velocities,
    arriving_irradiance,
):
    f32, bf16 = jnp.float32, jnp.bfloat16
    levels, columns, _, species = tracer_amounts.shape
    tile = thermal_anomaly.shape[1]
    gx, gy = lax.axis_size("gx"), lax.axis_size("gy")
    strips = ("gx", "gy")
    up = [(i, i + 1) for i in range(gx * gy - 1)]
    down = [(j, i) for i, j in up]
    gx_up = [(i, i + 1) for i in range(gx - 1)]
    gx_down = [(j, i) for i, j in gx_up]
    vmem = pl.BlockSpec(memory_space=pltpu.VMEM)
    smem = pl.BlockSpec(memory_space=pltpu.SMEM)
    hbm = pl.BlockSpec(memory_space=pltpu.HBM)

    mine = lax.axis_index("gy").astype(jnp.int32)
    place = jnp.stack([mine, jnp.zeros((), jnp.int32)])

    def halo_shape(k):
        low, high = chunk_rows(k)
        return jax.ShapeDtypeStruct((levels, SUB, high - low, species), bf16)

    rim_shape = jax.ShapeDtypeStruct((2 * 8, LANES), f32)
    *slices, rim_up, rim_down = pl.pallas_call(
        first_slice_kernel,
        out_shape=(halo_shape(0), halo_shape(0), rim_shape, rim_shape),
        in_specs=[smem, hbm] + [vmem] * 3,
        out_specs=(hbm, hbm, vmem, vmem),
        scratch_shapes=[pltpu.SemaphoreType.DMA((copy_count((0,)),))],
        compiler_params=pltpu.CompilerParams(vmem_limit_bytes=4 * 1024 * 1024),
        name="slice_first",
    )(place, tracer_amounts, zonal_transit_ratio, meridional_transit_ratio, thermal_anomaly)
    later = tuple(range(1, len(CHUNKS)))
    slices += pl.pallas_call(
        later_slice_kernel,
        out_shape=tuple(halo_shape(k) for k in later for _ in range(2)),
        in_specs=[smem, hbm],
        out_specs=(hbm,) * (2 * len(later)),
        scratch_shapes=[pltpu.SemaphoreType.DMA((copy_count(later),))],
        compiler_params=pltpu.CompilerParams(vmem_limit_bytes=4 * 1024 * 1024),
        name="slice_later",
    )(place, tracer_amounts)

    from_low = lax.ppermute(rim_up, "gx", gx_up)
    from_high = lax.ppermute(rim_down, "gx", gx_down)
    wests, easts = [], []
    for k in range(len(CHUNKS)):
        wests.append(lax.ppermute(slices[2 * k], strips, up))
        easts.append(lax.ppermute(slices[2 * k + 1], strips, down))

    packed = pl.pallas_call(
        pack_kernel,
        out_shape=jax.ShapeDtypeStruct((gy, FIELD_ROWS, LANES), f32),
        in_specs=[smem] + [vmem] * 8,
        out_specs=vmem,
        scratch_shapes=[pltpu.VMEM((4, tile + 16, LANES), f32)],
        compiler_params=pltpu.CompilerParams(vmem_limit_bytes=4 * 1024 * 1024),
        name="pack",
    )(
        place,
        zonal_transit_ratio,
        meridional_transit_ratio,
        moisture_ratio,
        stratum_depths,
        sun_elevation_factor,
        thermal_anomaly,
        from_low,
        from_high,
    )
    fields = lax.all_to_all(packed, "gy", split_axis=0, concat_axis=0, tiled=True)

    turned, classes = pl.pallas_call(
        turn_kernel,
        out_shape=(
            jax.ShapeDtypeStruct((levels, gy, LANES, LANES), bf16),
            jax.ShapeDtypeStruct((gy, columns, LANES), jnp.int32),
        ),
        in_specs=[vmem] * 3,
        out_specs=(vmem, vmem),
        compiler_params=pltpu.CompilerParams(vmem_limit_bytes=4 * 1024 * 1024),
        name="turn",
    )(fields, ground_cover_kind, particle_class_map)

    warmed = pl.pallas_call(
        warm_kernel,
        out_shape=jax.ShapeDtypeStruct(thermal_anomaly.shape, f32),
        in_specs=[smem] + [vmem] * 4,
        out_specs=vmem,
        scratch_shapes=[pltpu.VMEM((tile + 16, LANES), f32)],
        compiler_params=pltpu.CompilerParams(vmem_limit_bytes=4 * 1024 * 1024),
        name="warm",
    )(place, thermal_anomaly, from_low, from_high, fields)

    spread = jnp.asarray(spread_matrix(), bf16)
    table = jnp.concatenate([arid_extinction_table, swelling_factors], axis=1).T
    parts, rest = [], settling_velocities
    for _ in range(3):
        part = lax.reduce_precision(rest, 8, 7)
        parts.append(part.astype(bf16))
        rest = rest - part
    parts.append(jnp.zeros((LANES - 3 * settling_velocities.shape[0], species), bf16))
    speeds = jnp.concatenate(parts, axis=0)

    def run_chunk(k, out, heat):
        first, final = k == 0, k == len(CHUNKS) - 1
        operands = [
            place,
            arriving_irradiance,
            fields,
            classes,
            turned,
            spread,
            table,
            speeds,
            tracer_amounts,
            wests[k],
            easts[k],
        ]
        specs = [smem, smem] + [vmem] * 9
        heat_block = (levels * columns, LANES)
        out_shapes = [jax.ShapeDtypeStruct(tracer_amounts.shape, f32)]
        out_specs = [hbm]
        aliases = {}
        if not first:
            operands += [wests[k - 1], easts[k - 1]]
            specs += [vmem] * 2
            if final:
                operands += [wests[0], easts[0]]
                specs += [vmem] * 2
            aliases[len(operands)] = 0
            operands.append(out)
            specs.append(hbm)
        if final:
            out_shapes.append(jax.ShapeDtypeStruct(heat_block, f32))
            out_specs.append(vmem)
        else:
            if not first:
                aliases[len(operands)] = 1
                operands.append(heat)
                specs.append(hbm)
            out_shapes.append(jax.ShapeDtypeStruct((gy,) + heat_block, f32))
            out_specs.append(hbm)
        work = CHUNKS[k] * LANES * columns * levels * species
        span = LANES + 2 * MARGIN
        return pl.pallas_call(
            functools.partial(chunk_kernel, k),
            out_shape=tuple(out_shapes),
            in_specs=specs,
            out_specs=tuple(out_specs),
            scratch_shapes=[
                pltpu.VMEM((columns + 2 * SUB, span, LANES), f32),
                pltpu.VMEM((columns + 2 * SUB, span, LANES), f32),
                pltpu.VMEM((24, LANES + 2 * NEAR, LANES), f32),
                pltpu.VMEM((2, levels, columns, LANES, LANES), f32),
                pltpu.VMEM((columns, 8, LANES), f32),
                pltpu.VMEM((2, levels * columns, LANES), f32),
                pltpu.SemaphoreType.DMA((2, levels)),
                pltpu.SemaphoreType.DMA((2,)),
            ],
            input_output_aliases=aliases,
            compiler_params=pltpu.CompilerParams(vmem_limit_bytes=12 * 1024 * 1024),
            cost_estimate=pl.CostEstimate(
                flops=60 * work, transcendentals=0, bytes_accessed=8 * work
            ),
        )(*operands)

    out = heat = None
    for k in range(len(CHUNKS) - 1):
        out, heat = run_chunk(k, out, heat)
    returned = lax.all_to_all(heat, "gy", split_axis=0, concat_axis=0, tiled=True)
    out, own = run_chunk(len(CHUNKS) - 1, out, None)

    is_own = lax.broadcasted_iota(jnp.int32, (gy, 1, 1), 0) == mine
    returned = jnp.where(is_own, own[None], returned)
    returned = returned.reshape(gy, levels, columns, LANES).transpose(1, 0, 2, 3)
    return out, warmed + returned.reshape(thermal_anomaly.shape)


def solution(mesh):
    return jax.shard_map(
        per_device,
        mesh=mesh,
        in_specs=(
            P(None, ("gx", "gy"), None, None),
            P(None, "gx", "gy"),
            P(None, "gx", "gy"),
            P(None, "gx", "gy"),
            P(None, "gx", "gy"),
            P("gx", "gy"),
            P(None, "gx", "gy"),
            P(("gx", "gy"), None),
            P(("gx", "gy"), None),
            P(),
            P(),
            P(),
            P(),
        ),
        out_specs=(P(None, ("gx", "gy"), None, None), P(None, "gx", "gy")),
        check_vma=False,
    )
```

time: 128 us -> 149 us (1.16)
  the two profiles are of different devices: /device:TPU:0 before, /device:TPU:18 now
where the time goes in v1:
time: 149 us; the launch traced here: 148 us
  starting transfers between devices  49.2 us (33%)
  Pallas kernels  45.9 us (31%)
  waiting for transfers between devices  32.4 us (22%)
  local copies, waits for them, and re-layouts  16.4 us (11%)
  other arithmetic  2.95 us (2%)
    pallas_call x4, Pallas kernels, run_chunk(): pl.pallas_call(functools.partial(chunk_kernel, k), out_shape=tuple(out_sh...  40.7 us
    ppermute x4, waiting for transfers between devices, per_device(): easts.append(lax.ppermute(slices[2 * k + 1], strips, down))  29.5 us
    ppermute x4, starting transfers between devices, per_device(): easts.append(lax.ppermute(slices[2 * k + 1], strips, down))  16.7 us
    unnamed x60, local copies, waits for them, and re-layouts  16.3 us
    ppermute x4, starting transfers between devices, per_device(): wests.append(lax.ppermute(slices[2 * k], strips, up))  10.7 us
    all_to_all x1, starting transfers between devices, per_device(): lax.all_to_all(heat, 'gy', split_axis=0, concat_axis=0, tiled=True)  8.64 us
    all_to_all x1, starting transfers between devices, per_device(): lax.all_to_all(packed, 'gy', split_axis=0, concat_axis=0, tiled=True)  7.55 us
    ppermute x1, starting transfers between devices, per_device(): from_high = lax.ppermute(rim_down, 'gx', gx_down)  3.64 us
  transfers between devices with their start and end apart: 12, of which 2 were waited for; matrix products, arithmetic and copies ran while one was open for 1% of the time, Pallas kernels for 30%

profile of v1, /device:TPU:18, one launch (start us, length us, event | category | flops | bytes accessed | tf_op | source)
XLA Modules:
  0.0 147.9 jit_solution(4268492001551398131)
XLA Ops:
  0.7 2.2 %copy-done = bf16[2,8,1024,128]{3,2,1,0:T(8,128)(2,1)S(1)} copy-done((bf16[2,8,1024,128]{3,2,1,0:T(8,128)(2,1)S(1)}, bf16[2,8,1024,128]{3,2,1,0:T(8,128)(2,1)}, u32[]{:S(2)}) %copy-start) | copy-done | bytes 4194328
  6.4 3.8 %collective-permute-start.6 = (bf16[2,3,288,128]{3,2,1,0:T(8,128)(2,1)S(1)}, bf16[2,3,288,128]{3,2,1,0:T(8,128)(2,1)S(1)}, u32[]{:S(2)}, u32[]{:S(2)}) collective-permute-start(bf16[2,3,288,128]{3,2,1,0:T(8,128)(2,1)S(1)} %get-tuple-element.30), channel_id=1, source_target_pairs={{0,1},{1,2},{2,3},{3,4},{4,5},{5,6},{6,7},{7,8},{8,9},{9,10},{10,1... | collective-permute-start | bytes 1327112 | tf_op jit(solution)/shard_map/ppermute | solution.py:454
  10.2 2.0 %slice_later.1 = (bf16[2,3,384,128]{3,2,1,0:T(8,128)(2,1)}, bf16[2,3,384,128]{3,2,1,0:T(8,128)(2,1)}, bf16[2,3,256,128]{3,2,1,0:T(8,128)(2,1)}, bf16[2,3,256,128...) custom-call(s32[2]{0:T(128)S(1)} %pad_add_fusion.place.refs_0_, ...), custom_call_target="tpu_custom_call" | custom-call | tf_op jit(solution)/shard_map/slice_later/pallas_call | solution.py:440
  12.2 2.9 %collective-permute-start.8 = (bf16[2,3,384,128]{3,2,1,0:T(8,128)(2,1)}, bf16[2,3,384,128]{3,2,1,0:T(8,128)(2,1)}, u32[]{:S(2)}, u32[]{:S(2)}) collective-permute-start(bf16[2,3,384,128]{3,2,1,0:T(8,128)(2,1)} %get-tuple-element.32), channel_id=1, source_target_pairs={{0,1},{1,2},{2,3},{3,4},{4,5},{5,6},{6,7},{7,8},{8,9},{9,10},{10,1... | collective-permute-start | bytes 1769480 | tf_op jit(solution)/shard_map/ppermute | solution.py:454
  15.1 3.8 %collective-permute-start.9 = (bf16[2,3,384,128]{3,2,1,0:T(8,128)(2,1)}, bf16[2,3,384,128]{3,2,1,0:T(8,128)(2,1)}, u32[]{:S(2)}, u32[]{:S(2)}) collective-permute-start(bf16[2,3,384,128]{3,2,1,0:T(8,128)(2,1)} %get-tuple-element.33), channel_id=1, source_target_pairs={{1,0},{2,1},{3,2},{4,3},{5,4},{6,5},{7,6},{8,7},{9,8},{10,9},{11,1... | collective-permute-start | bytes 1769480 | tf_op jit(solution)/shard_map/ppermute | solution.py:455
  19.0 1.9 %collective-permute-start = (f32[16,128]{1,0:T(8,128)S(1)}, f32[16,128]{1,0:T(8,128)S(1)}, u32[]{:S(2)}, u32[]{:S(2)}) collective-permute-start(f32[16,128]{1,0:T(8,128)S(1)} %get-tuple-element.22), channel_id=1, source_target_pairs={{0,8},{8,16},{16,24},{24,32},{32,40},{40,48},{48,56},{56,64},{64,7... | collective-permute-start | bytes 24584 | tf_op jit(solution)/shard_map/ppermute | solution.py:450
  20.9 3.6 %collective-permute-start.1 = (f32[16,128]{1,0:T(8,128)S(1)}, f32[16,128]{1,0:T(8,128)S(1)}, u32[]{:S(2)}, u32[]{:S(2)}) collective-permute-start(f32[16,128]{1,0:T(8,128)S(1)} %get-tuple-element.23), channel_id=1, source_target_pairs={{8,0},{16,8},{24,16},{32,24},{40,32},{48,40},{56,48},{64,56},{72,6... | collective-permute-start | bytes 24584 | tf_op jit(solution)/shard_map/ppermute | solution.py:451
  24.5 2.0 %collective-permute-start.4 = (bf16[2,3,256,128]{3,2,1,0:T(8,128)(2,1)}, bf16[2,3,256,128]{3,2,1,0:T(8,128)(2,1)S(1)}, u32[]{:S(2)}, u32[]{:S(2)}) collective-permute-start(bf16[2,3,256,128]{3,2,1,0:T(8,128)(2,1)} %get-tuple-element.28), channel_id=1, source_target_pairs={{0,1},{1,2},{2,3},{3,4},{4,5},{5,6},{6,7},{7,8},{8,9},{9,10},{10,1... | collective-permute-start | bytes 1179656 | tf_op jit(solution)/shard_map/ppermute | solution.py:454
  26.6 4.7 %collective-permute-start.5 = (bf16[2,3,256,128]{3,2,1,0:T(8,128)(2,1)}, bf16[2,3,256,128]{3,2,1,0:T(8,128)(2,1)}, u32[]{:S(2)}, u32[]{:S(2)}) collective-permute-start(bf16[2,3,256,128]{3,2,1,0:T(8,128)(2,1)} %get-tuple-element.29), channel_id=1, source_target_pairs={{1,0},{2,1},{3,2},{4,3},{5,4},{6,5},{7,6},{8,7},{9,8},{10,9},{11,1... | collective-permute-start | bytes 1179656 | tf_op jit(solution)/shard_map/ppermute | solution.py:455
  31.4 1.4 pack.1
  33.4 7.6 %all-to-all-start = ((f32[8,96,128]{2,1,0:T(8,128)}), f32[8,96,128]{2,1,0:T(8,128)S(1)}, u32[]{:S(2)}, u32[]{:S(2)}) async-start(f32[8,96,128]{2,1,0:T(8,128)} %pack.1), calls=%async_computation | async-start | bytes 786432 | tf_op jit(solution)/shard_map/all_to_all | solution.py:476
  41.0 2.8 %collective-permute-done.6.refs_9_.refs_11_.refs_13_ = bf16[2,3,288,128]{3,2,1,0:T(8,128)(2,1)S(1)} collective-permute-done((bf16[2,3,288,128]{3,2,1,0:T(8,128)(2,1)S(1)}, bf16[2,3,288,128]{3,2,1,0:T(8,128)(2,1)S(1)}, u32[]{:S(2)}, u32[]{:S(2)}) %collective-permute-start.6) | collective-permute-done | bytes 442400 | tf_op jit(solution)/shard_map/ppermute | solution.py:454
  43.8 3.4 %collective-permute-start.7 = (bf16[2,3,288,128]{3,2,1,0:T(8,128)(2,1)S(1)}, bf16[2,3,288,128]{3,2,1,0:T(8,128)(2,1)S(1)}, u32[]{:S(2)}, u32[]{:S(2)}) collective-permute-start(bf16[2,3,288,128]{3,2,1,0:T(8,128)(2,1)S(1)} %get-tuple-element.31), channel_id=1, source_target_pairs={{1,0},{2,1},{3,2},{4,3},{5,4},{6,5},{7,6},{8,7},{9,8},{10,9},{11,1... | collective-permute-start | bytes 1327112 | tf_op jit(solution)/shard_map/ppermute | solution.py:455
  47.4 29.5 %collective-permute-done.7.refs_10_.refs_12_.refs_14_ = bf16[2,3,288,128]{3,2,1,0:T(8,128)(2,1)S(1)} collective-permute-done((bf16[2,3,288,128]{3,2,1,0:T(8,128)(2,1)S(1)}, bf16[2,3,288,128]{3,2,1,0:T(8,128)(2,1)S(1)}, u32[]{:S(2)}, u32[]{:S(2)}) %collective-permute-start.7) | collective-permute-done | bytes 442400 | tf_op jit(solution)/shard_map/ppermute | solution.py:455
  76.9 1.9 %collective-permute-start.2 = (bf16[2,3,112,128]{3,2,1,0:T(8,128)(2,1)}, bf16[2,3,112,128]{3,2,1,0:T(8,128)(2,1)}, u32[]{:S(2)}, u32[]{:S(2)}) collective-permute-start(bf16[2,3,112,128]{3,2,1,0:T(8,128)(2,1)} %copy-done.26), channel_id=1, source_target_pairs={{0,1},{1,2},{2,3},{3,4},{4,5},{5,6},{6,7},{7,8},{8,9},{9,10},{10,1... | collective-permute-start | bytes 516104 | tf_op jit(solution)/shard_map/ppermute | solution.py:454
  78.8 4.8 %collective-permute-start.3 = (bf16[2,3,112,128]{3,2,1,0:T(8,128)(2,1)}, bf16[2,3,112,128]{3,2,1,0:T(8,128)(2,1)}, u32[]{:S(2)}, u32[]{:S(2)}) collective-permute-start(bf16[2,3,112,128]{3,2,1,0:T(8,128)(2,1)} %copy-done.25), channel_id=1, source_target_pairs={{1,0},{2,1},{3,2},{4,3},{5,4},{6,5},{7,6},{8,7},{9,8},{10,9},{11,1... | collective-permute-start | bytes 516104 | tf_op jit(solution)/shard_map/ppermute | solution.py:455
  86.1 2.2 %copy-done.1 = bf16[2,8,1024,128]{3,2,1,0:T(8,128)(2,1)S(1)} copy-done((bf16[2,8,1024,128]{3,2,1,0:T(8,128)(2,1)S(1)}, bf16[2,8,1024,128]{3,2,1,0:T(8,128)(2,1)}, u32[]{:S(2)}) %copy-start.1) | copy-done | bytes 4194328
  89.0 9.4 %shard_map.149 = (f32[2,8,1024,128]{3,2,1,0:T(8,128)}, f32[8,16,128]{2,1,0:T(8,128)S(1)}) custom-call(s32[2]{0:T(128)S(1)} %pad_add_fusion.place.refs_0_, f32[4]{0:T(128)S(1)} %copy-done.24, f32[8,96,128]{2,1,0:T(8,128)S(1)} %all-to-all-done.fields.refs_2_, s32[8,8,128]{2,1,0:T(8,128)S(1)} %get-tuple-element.24.refs_3_, ...), custom_call_target="tpu_custom_call" | custom-call | flops 31457280 | bytes 4194304 | tf_op jit(solution)/shard_map/pallas_call | solution.py:551
  98.4 14.8 %shard_map.150 = (f32[2,8,1024,128]{3,2,1,0:T(8,128)}, f32[8,16,128]{2,1,0:T(8,128)S(1)}) custom-call(s32[2]{0:T(128)S(1)} %pad_add_fusion.place.refs_0_, f32[4]{0:T(128)S(1)} %copy-done.24, f32[8,96,128]{2,1,0:T(8,128)S(1)} %all-to-all-done.fields.refs_2_, ...), custom_call_target="tpu_custom_call", output_to_operand_aliasing={{0}: (13, {}), {1}: (14, {})} | custom-call | flops 47185920 | bytes 6291456 | tf_op jit(solution)/shard_map/pallas_call | solution.py:551
  113.2 10.6 %shard_map.151 = (f32[2,8,1024,128]{3,2,1,0:T(8,128)}, f32[8,16,128]{2,1,0:T(8,128)S(1)}) custom-call(s32[2]{0:T(128)S(1)} %pad_add_fusion.place.refs_0_, f32[4]{0:T(128)S(1)} %copy-done.24, f32[8,96,128]{2,1,0:T(8,128)S(1)} %all-to-all-done.fields.refs_2_, ...), custom_call_target="tpu_custom_call", output_to_operand_aliasing={{0}: (13, {}), {1}: (14, {})} | custom-call | flops 31457280 | bytes 4194304 | tf_op jit(solution)/shard_map/pallas_call | solution.py:551
  124.4 8.6 %all-to-all-start.1 = ((f32[8,16,128]{2,1,0:T(8,128)}), f32[8,16,128]{2,1,0:T(8,128)}, u32[]{:S(2)}, u32[]{:S(2)}) async-start(f32[8,16,128]{2,1,0:T(8,128)} %copy-done.6), calls=%async_computation.1 | async-start | bytes 131072 | tf_op jit(solution)/shard_map/all_to_all | solution.py:576
  136.6 2.2 %copy-done.2 = bf16[2,8,1024,128]{3,2,1,0:T(8,128)(2,1)S(1)} copy-done((bf16[2,8,1024,128]{3,2,1,0:T(8,128)(2,1)S(1)}, bf16[2,8,1024,128]{3,2,1,0:T(8,128)(2,1)}, u32[]{:S(2)}) %copy-start.2) | copy-done | bytes 4194328
  140.3 6.0 %shard_map.152 = (f32[2,8,1024,128]{3,2,1,0:T(8,128)}, f32[16,128]{1,0:T(8,128)S(1)}) custom-call(s32[2]{0:T(128)S(1)} %pad_add_fusion.place.refs_0_, f32[4]{0:T(128)S(1)} %copy-done.24, f32[8,96,128]{2,1,0:T(8,128)S(1)} %all-to-all-done.fields.refs_2_, s32[8,8,128]{2,1,0:T(8,128)S(1)} %copy-done.11, ...), custom_call_target="tpu_custom_call", output_to_operand_aliasing={{0}: (15, {})} | custom-call | flops 15728640 | bytes 2097152 | tf_op jit(solution)/shard_map/pallas_call | solution.py:551
  146.3 1.6 %bitcast_add_fusion = f32[2,64,128]{2,1,0:T(8,128)} fusion(f32[2,64,128]{2,1,0:T(8,128)} %copy-done.16, f32[8,16,128]{2,1,0:T(8,128)} %all-to-all-done.1, f32[16,128]{1,0:T(8,128)S(1)} %get-tuple-element.40, pred[8]{0:T(512)(128)(4,1)} %iota_compare_fusion), kind=kLoop, calls=%fused_computation | loop fusion | flops 32768 | bytes 204808 | tf_op jit(solution)/shard_map/add | solution.py:582
  (77 shorter events, 13.1 us)
Async XLA Ops:
  0.6 85.4 %copy-start.24 = (f32[4]{0:T(128)S(1)}, f32[4]{0:T(128)}, u32[]{:S(2)}) copy-start(f32[4]{0:T(128)} %refs_1_.7) | copy-start | bytes 52
  5.4 25.9 %copy-start.8 = (f32[2,64,128]{2,1,0:T(8,128)S(1)}, f32[2,64,128]{2,1,0:T(8,128)}, u32[]{:S(2)}) copy-start(f32[2,64,128]{2,1,0:T(8,128)} %warmth.5) | copy-start | bytes 196612
  5.4 25.9 %copy-start.13 = (f32[2,64,128]{2,1,0:T(8,128)S(1)}, f32[2,64,128]{2,1,0:T(8,128)}, u32[]{:S(2)}) copy-start(f32[2,64,128]{2,1,0:T(8,128)} %u.3) | copy-start | bytes 196612
  5.4 25.9 %copy-start.15 = (f32[2,64,128]{2,1,0:T(8,128)S(1)}, f32[2,64,128]{2,1,0:T(8,128)}, u32[]{:S(2)}) copy-start(f32[2,64,128]{2,1,0:T(8,128)} %v.3) | copy-start | bytes 196612
  5.4 25.9 %copy-start.17 = (f32[2,64,128]{2,1,0:T(8,128)S(1)}, f32[2,64,128]{2,1,0:T(8,128)}, u32[]{:S(2)}) copy-start(f32[2,64,128]{2,1,0:T(8,128)} %moisture.1) | copy-start | bytes 196612
  5.4 25.9 %copy-start.18 = (f32[2,64,128]{2,1,0:T(8,128)S(1)}, f32[2,64,128]{2,1,0:T(8,128)}, u32[]{:S(2)}) copy-start(f32[2,64,128]{2,1,0:T(8,128)} %depth.1) | copy-start | bytes 196612
  5.5 25.9 %copy-start.23 = (f32[64,128]{1,0:T(8,128)S(1)}, f32[64,128]{1,0:T(8,128)}, u32[]{:S(2)}) copy-start(f32[64,128]{1,0:T(8,128)} %sun.1) | copy-start | bytes 98308
  5.5 41.8 %copy-start.29 = (f32[24,128]{1,0:T(8,128)S(1)}, f32[24,128]{1,0:T(8,128)}, u32[]{:S(2)}) copy-start(f32[24,128]{1,0:T(8,128)} %param.25) | copy-start | bytes 36868
  5.5 78.2 %copy-start.27 = (bf16[128,64]{0,1:T(8,128)(2,1)S(1)}, bf16[128,64]{0,1:T(8,128)(2,1)}, u32[]{:S(2)}) copy-start(bf16[128,64]{0,1:T(8,128)(2,1)} %param.24) | copy-start | bytes 49156
  5.5 78.2 %copy-start.28 = (bf16[128,64]{0,1:T(8,128)(2,1)S(1)}, bf16[128,64]{0,1:T(8,128)(2,1)}, u32[]{:S(2)}) copy-start(bf16[128,64]{0,1:T(8,128)(2,1)} %param.23) | copy-start | bytes 49156
  5.5 80.5 %copy-start.3 = (bf16[20,128,256]{2,1,0:T(8,128)(2,1)S(1)}, bf16[20,128,256]{2,1,0:T(8,128)(2,1)}, u32[]{:S(2)}) copy-start(bf16[20,128,256]{2,1,0:T(8,128)(2,1)} %constant.10.clone.refs_5_) | copy-start | bytes 3932164
  6.4 37.4 %collective-permute-start.6 = (bf16[2,3,288,128]{3,2,1,0:T(8,128)(2,1)S(1)}, bf16[2,3,288,128]{3,2,1,0:T(8,128)(2,1)S(1)}, u32[]{:S(2)}, u32[]{:S(2)}) collective-permute-start(bf16[2,3,288,128]{3,2,1,0:T(8,128)(2,1)S(1)} %get-tuple-element.30), channel_id=1, source_target_pairs={{0,1},{1,2},{2,3},{3,4},{4,5},{5,6},{6,7},{7,8},{8,9},{9,10},{10,1... | collective-permute-start | bytes 1327112 | tf_op jit(solution)/shard_map/ppermute | solution.py:454
  12.2 66.6 %collective-permute-start.8 = (bf16[2,3,384,128]{3,2,1,0:T(8,128)(2,1)}, bf16[2,3,384,128]{3,2,1,0:T(8,128)(2,1)}, u32[]{:S(2)}, u32[]{:S(2)}) collective-permute-start(bf16[2,3,384,128]{3,2,1,0:T(8,128)(2,1)} %get-tuple-element.32), channel_id=1, source_target_pairs={{0,1},{1,2},{2,3},{3,4},{4,5},{5,6},{6,7},{7,8},{8,9},{9,10},{10,1... | collective-permute-start | bytes 1769480 | tf_op jit(solution)/shard_map/ppermute | solution.py:454
  15.1 83.2 %collective-permute-start.9 = (bf16[2,3,384,128]{3,2,1,0:T(8,128)(2,1)}, bf16[2,3,384,128]{3,2,1,0:T(8,128)(2,1)}, u32[]{:S(2)}, u32[]{:S(2)}) collective-permute-start(bf16[2,3,384,128]{3,2,1,0:T(8,128)(2,1)} %get-tuple-element.33), channel_id=1, source_target_pairs={{1,0},{2,1},{3,2},{4,3},{5,4},{6,5},{7,6},{8,7},{9,8},{10,9},{11,1... | collective-permute-start | bytes 1769480 | tf_op jit(solution)/shard_map/ppermute | solution.py:455
  19.0 5.6 %collective-permute-start = (f32[16,128]{1,0:T(8,128)S(1)}, f32[16,128]{1,0:T(8,128)S(1)}, u32[]{:S(2)}, u32[]{:S(2)}) collective-permute-start(f32[16,128]{1,0:T(8,128)S(1)} %get-tuple-element.22), channel_id=1, source_target_pairs={{0,8},{8,16},{16,24},{24,32},{32,40},{40,48},{48,56},{56,64},{64,7... | collective-permute-start | bytes 24584 | tf_op jit(solution)/shard_map/ppermute | solution.py:450
  20.9 5.7 %collective-permute-start.1 = (f32[16,128]{1,0:T(8,128)S(1)}, f32[16,128]{1,0:T(8,128)S(1)}, u32[]{:S(2)}, u32[]{:S(2)}) collective-permute-start(f32[16,128]{1,0:T(8,128)S(1)} %get-tuple-element.23), channel_id=1, source_target_pairs={{8,0},{16,8},{24,16},{32,24},{40,32},{48,40},{56,48},{64,56},{72,6... | collective-permute-start | bytes 24584 | tf_op jit(solution)/shard_map/ppermute | solution.py:451
  24.5 88.6 %collective-permute-start.4 = (bf16[2,3,256,128]{3,2,1,0:T(8,128)(2,1)}, bf16[2,3,256,128]{3,2,1,0:T(8,128)(2,1)S(1)}, u32[]{:S(2)}, u32[]{:S(2)}) collective-permute-start(bf16[2,3,256,128]{3,2,1,0:T(8,128)(2,1)} %get-tuple-element.28), channel_id=1, source_target_pairs={{0,1},{1,2},{2,3},{3,4},{4,5},{5,6},{6,7},{7,8},{8,9},{9,10},{10,1... | collective-permute-start | bytes 1179656 | tf_op jit(solution)/shard_map/ppermute | solution.py:454
  26.6 86.6 %collective-permute-start.5 = (bf16[2,3,256,128]{3,2,1,0:T(8,128)(2,1)}, bf16[2,3,256,128]{3,2,1,0:T(8,128)(2,1)}, u32[]{:S(2)}, u32[]{:S(2)}) collective-permute-start(bf16[2,3,256,128]{3,2,1,0:T(8,128)(2,1)} %get-tuple-element.29), channel_id=1, source_target_pairs={{1,0},{2,1},{3,2},{4,3},{5,4},{6,5},{7,6},{8,7},{9,8},{10,9},{11,1... | collective-permute-start | bytes 1179656 | tf_op jit(solution)/shard_map/ppermute | solution.py:455
  33.4 50.9 %all-to-all-start = ((f32[8,96,128]{2,1,0:T(8,128)}), f32[8,96,128]{2,1,0:T(8,128)S(1)}, u32[]{:S(2)}, u32[]{:S(2)}) async-start(f32[8,96,128]{2,1,0:T(8,128)} %pack.1), calls=%async_computation | async-start | bytes 786432 | tf_op jit(solution)/shard_map/all_to_all | solution.py:476
  43.8 33.1 %collective-permute-start.7 = (bf16[2,3,288,128]{3,2,1,0:T(8,128)(2,1)S(1)}, bf16[2,3,288,128]{3,2,1,0:T(8,128)(2,1)S(1)}, u32[]{:S(2)}, u32[]{:S(2)}) collective-permute-start(bf16[2,3,288,128]{3,2,1,0:T(8,128)(2,1)S(1)} %get-tuple-element.31), channel_id=1, source_target_pairs={{1,0},{2,1},{3,2},{4,3},{5,4},{6,5},{7,6},{8,7},{9,8},{10,9},{11,1... | collective-permute-start | bytes 1327112 | tf_op jit(solution)/shard_map/ppermute | solution.py:455
  76.9 59.7 %collective-permute-start.2 = (bf16[2,3,112,128]{3,2,1,0:T(8,128)(2,1)}, bf16[2,3,112,128]{3,2,1,0:T(8,128)(2,1)}, u32[]{:S(2)}, u32[]{:S(2)}) collective-permute-start(bf16[2,3,112,128]{3,2,1,0:T(8,128)(2,1)} %copy-done.26), channel_id=1, source_target_pairs={{0,1},{1,2},{2,3},{3,4},{4,5},{5,6},{6,7},{7,8},{8,9},{9,10},{10,1... | collective-permute-start | bytes 516104 | tf_op jit(solution)/shard_map/ppermute | solution.py:454
  78.8 57.8 %collective-permute-start.3 = (bf16[2,3,112,128]{3,2,1,0:T(8,128)(2,1)}, bf16[2,3,112,128]{3,2,1,0:T(8,128)(2,1)}, u32[]{:S(2)}, u32[]{:S(2)}) collective-permute-start(bf16[2,3,112,128]{3,2,1,0:T(8,128)(2,1)} %copy-done.25), channel_id=1, source_target_pairs={{1,0},{2,1},{3,2},{4,3},{5,4},{6,5},{7,6},{8,7},{9,8},{10,9},{11,1... | collective-permute-start | bytes 516104 | tf_op jit(solution)/shard_map/ppermute | solution.py:455
  86.0 27.2 %copy-start.10 = (s32[8,8,128]{2,1,0:T(8,128)}, s32[8,8,128]{2,1,0:T(8,128)S(1)}, u32[]{:S(2)}) copy-start(s32[8,8,128]{2,1,0:T(8,128)S(1)} %get-tuple-element.24.refs_3_) | copy-start | bytes 98308
  124.4 21.9 %all-to-all-start.1 = ((f32[8,16,128]{2,1,0:T(8,128)}), f32[8,16,128]{2,1,0:T(8,128)}, u32[]{:S(2)}, u32[]{:S(2)}) async-start(f32[8,16,128]{2,1,0:T(8,128)} %copy-done.6), calls=%async_computation.1 | async-start | bytes 131072 | tf_op jit(solution)/shard_map/all_to_all | solution.py:576
  (18 other events, 45.1 us)

commit v2 on v1

--- a/solution.py
+++ b/solution.py
@@ -63,21 +63,23 @@
 
 def slice_copies(chunks, place, tracer, outs, sems):
     mine = place[0]
+    odd = lax.rem(mine, 2)
     blocks = tracer.shape[2] // LANES
     columns = tracer.shape[1]
     copies = []
     for n, k in enumerate(chunks):
         low, top = chunk_rows(k)
-        for side in range(2):
-            target = lax.rem(mine + (1 if side == 0 else blocks - 1), blocks)
-            first = columns - SUB if side == 0 else 0
+        for swap in range(2):
+            upward = odd if swap else 1 - odd
+            target = lax.rem(mine + 2 * upward - 1 + blocks, blocks)
+            first = upward * (columns - SUB)
             for a, b in slice_pieces(low, top):
                 block = lax.rem(target + 1 + (a // LANES) + blocks, blocks)
                 row = pl.multiple_of(block * LANES + a % LANES, MARGIN)
                 copies.append(
                     pltpu.make_async_copy(
-                        tracer.at[:, first : first + SUB, pl.ds(row, b - a), :],
-                        outs[2 * n + side].at[:, :, a - low : b - low, :],
+                        tracer.at[:, pl.ds(first, SUB), pl.ds(row, b - a), :],
+                        outs[2 * n + swap].at[:, :, a - low : b - low, :],
                         sems.at[len(copies)],
                     )
                 )
@@ -88,22 +90,26 @@
     return sum(2 * len(slice_pieces(*chunk_rows(k))) for k in chunks)
 
 
-def first_slice_kernel(place, tracer, u, v, warmth, up, down, rim_up, rim_down, sems):
-    copies = slice_copies((0,), place, tracer, (up, down), sems)
+def first_slice_kernel(place, tracer, u, v, warmth, out_0, out_1, rim_0, rim_1, sems):
+    copies = slice_copies((0,), place, tracer, (out_0, out_1), sems)
     for copy in copies:
         copy.start()
     span = u.shape[1]
+    odd = place[2] == 1
+
+    def put(at, low, high):
+        n = low.shape[0]
+        rim_0[at : at + n, :] = jnp.where(odd, low, high)
+        rim_1[at : at + n, :] = jnp.where(odd, high, low)
+
     for f in range(4):
         source = (u, v)[f // 2]
-        rim_up[RIM * f : RIM * (f + 1), :] = source[f % 2, span - RIM : span, :]
-        rim_down[RIM * f : RIM * (f + 1), :] = source[f % 2, 0:RIM, :]
+        put(RIM * f, source[f % 2, 0:RIM, :], source[f % 2, span - RIM : span, :])
     for level in range(2):
-        at = 4 * RIM + level
-        rim_up[at : at + 1, :] = warmth[level, span - 1 : span, :]
-        rim_down[at : at + 1, :] = warmth[level, 0:1, :]
+        put(4 * RIM + level, warmth[level, 0:1, :], warmth[level, span - 1 : span, :])
     at = 4 * RIM + 2
-    rim_up[at:, :] = jnp.zeros((rim_up.shape[0] - at, LANES), jnp.float32)
-    rim_down[at:, :] = jnp.zeros((rim_up.shape[0] - at, LANES), jnp.float32)
+    for rim in (rim_0, rim_1):
+        rim[at:, :] = jnp.zeros((rim.shape[0] - at, LANES), jnp.float32)
     for copy in copies:
         copy.wait()
 
@@ -117,8 +123,14 @@
         copy.wait()
 
 
-def pack_kernel(place, u, v, moisture, depth, sun, warmth, low, high, out, ext):
+def rims_of(place, rim_0, rim_1):
+    odd = place[2] == 1
+    return jnp.where(odd, rim_0[...], rim_1[...]), jnp.where(odd, rim_1[...], rim_0[...])
+
+
+def pack_kernel(place, u, v, moisture, depth, sun, warmth, rim_0, rim_1, out, ext):
     mine = place[0]
+    low, high = rims_of(place, rim_0, rim_1)
     parts = u.shape[1] // 8
     for f in range(4):
         source = (u, v)[f // 2]
@@ -162,8 +174,9 @@
             turned[level, block] = jnp.concatenate(parts, axis=0).T.astype(jnp.bfloat16)
 
 
-def warm_kernel(place, warmth, low, high, fields, out, ext):
+def warm_kernel(place, warmth, rim_0, rim_1, fields, out, ext):
     mine = place[0]
+    low, high = rims_of(place, rim_0, rim_1)
     tiles = fields.shape[0]
     span = warmth.shape[1]
     lane = lax.broadcasted_iota(jnp.int32, (span, LANES), 1)
@@ -183,6 +196,40 @@
         out[level] = here + SPREAD_FACTOR * laplace
 
 
+def own_kernel(place, tracer, fields, classes, turned, window, own_fields, own_classes, lhs, sems):
+    mine = place[0]
+    blocks = fields.shape[0]
+    row = pl.multiple_of(mine * LANES, LANES)
+    low = pl.multiple_of(jnp.maximum(row - MARGIN, 0), MARGIN)
+    high = pl.multiple_of(jnp.minimum(row + LANES, tracer.shape[2] - MARGIN), MARGIN)
+    copies = []
+    for source, at, n in ((low, 0, MARGIN), (row, MARGIN, LANES), (high, MARGIN + LANES, MARGIN)):
+        copies.append(
+            pltpu.make_async_copy(
+                tracer.at[:, :, pl.ds(source, n), :],
+                window.at[:, :, at : at + n, :],
+                sems.at[len(copies)],
+            )
+        )
+    for copy in copies:
+        copy.start()
+    own_fields[...] = fields[mine]
+    own_classes[...] = classes[mine]
+    for level in range(2):
+        lhs[level] = block_lhs(turned, level, mine, blocks)
+    for copy in copies:
+        copy.wait()
+
+
+def block_lhs(turned, level, block, blocks):
+    low = turned[level, jnp.maximum(block - 1, 0), LANES - MARGIN :, :].astype(jnp.float32)
+    high = turned[level, jnp.minimum(block + 1, blocks - 1), :MARGIN, :].astype(jnp.float32)
+    low = low * jnp.where(block != 0, 1.0, 0.0)
+    high = high * jnp.where(block != blocks - 1, 1.0, 0.0)
+    ends = [low.astype(jnp.bfloat16), high.astype(jnp.bfloat16)]
+    return jnp.concatenate([ends[0], turned[level, block], ends[1]], axis=0)
+
+
 def row_blocks(first, count, size):
     return [(r, min(size, first + count - r)) for r in range(first, first + count, size)]
 
@@ -191,9 +238,9 @@
     first, final = k == 0, k == len(CHUNKS) - 1
     count = CHUNKS[k]
     refs = list(refs)
-    place, sunlight, fields, classes, turned, spread, table, speeds, tracer = refs[:9]
+    place, sunlight, spread, table, speeds, fields, classes, turned, tracer = refs[:9]
     del refs[:9]
-    west, east = refs[:2]
+    halos = refs[:2]
     del refs[:2]
     before = (None, None)
     if not first:
@@ -212,8 +259,9 @@
     columns = 8
     wide = columns + 2 * SUB
     mine, z = place[0], place[1]
-    blocks = fields.shape[0]
-    grid_rows = tracer.shape[2]
+    parity = lax.rem(mine, 2)
+    blocks = out.shape[2] // LANES
+    grid_rows = out.shape[2]
     top = MARGIN + LANES
 
     sublane = lax.broadcasted_iota(jnp.int32, (8, LANES), 0)
@@ -238,6 +286,9 @@
             these.append(pltpu.make_async_copy(warm.at[slot], heat.at[block], heat_sems.at[slot]))
         return these
 
+    def field_row(block, at):
+        return fields[at : at + 1, :] if final else fields[block, at : at + 1, :]
+
     def step(source, c, i, r0, n):
         here = source[c, r0 : r0 + n, :]
         u = coef[2 * i, r0 - NEAR : r0 - NEAR + n, :]
@@ -254,8 +305,6 @@
         row = pl.multiple_of(block * LANES, LANES)
         low_row = pl.multiple_of(jnp.maximum(row - MARGIN, 0), MARGIN)
         high_row = pl.multiple_of(jnp.minimum(row + LANES, grid_rows - MARGIN), MARGIN)
-        low_block = jnp.maximum(block - 1, 0)
-        high_block = jnp.minimum(block + 1, blocks - 1)
         has_low = jnp.where(block != 0, 1.0, 0.0)
         has_high = jnp.where(block != blocks - 1, 1.0, 0.0)
 
@@ -267,12 +316,11 @@
                     copy.wait()
 
         for level in (1, 0):
-            low_margin = wide_of(turned[level, low_block, LANES - MARGIN :, :]) * has_low
-            high_margin = wide_of(turned[level, high_block, :MARGIN, :]) * has_high
-            middle = turned[level, block]
-            lhs = jnp.concatenate(
-                [low_margin.astype(jnp.bfloat16), middle, high_margin.astype(jnp.bfloat16)], axis=0
-            )
+            lhs = turned[level] if final else block_lhs(turned, level, block, blocks)
+            for c in range(wide - 2):
+                both = jnp.dot(lhs, spread[c], preferred_element_type=jnp.float32)
+                coef[2 * c] = both[NEAR : top + NEAR, :LANES]
+                coef[2 * c + 1] = both[NEAR : top + NEAR, LANES:]
 
             def widen(at, low, head, tail, high):
                 even[at, NEAR:MARGIN, :] = wide_of(low)[NEAR:, :] * has_low
@@ -280,26 +328,41 @@
                 even[at, 2 * MARGIN : top, :] = wide_of(tail)
                 even[at, top : top + NEAR, :] = wide_of(high)[:NEAR, :] * has_high
 
-            for x in range(columns):
-                widen(
-                    SUB + x,
-                    tracer[level, x, pl.ds(low_row, MARGIN), :],
-                    tracer[level, x, pl.ds(row, MARGIN), :],
-                    tracer[level, x, pl.ds(pl.multiple_of(row + MARGIN, MARGIN), LANES - MARGIN), :],
-                    tracer[level, x, pl.ds(high_row, MARGIN), :],
-                )
+            def widen_column(x, carry):
+                if final:
+                    parts = [
+                        tracer[level, x, r : r + n, :]
+                        for r, n in (
+                            (0, MARGIN),
+                            (MARGIN, MARGIN),
+                            (2 * MARGIN, LANES - MARGIN),
+                            (top, MARGIN),
+                        )
+                    ]
+                else:
+                    inner = pl.multiple_of(row + MARGIN, MARGIN)
+                    parts = [
+                        tracer[level, x, pl.ds(low_row, MARGIN), :],
+                        tracer[level, x, pl.ds(row, MARGIN), :],
+                        tracer[level, x, pl.ds(inner, LANES - MARGIN), :],
+                        tracer[level, x, pl.ds(high_row, MARGIN), :],
+                    ]
+                widen(SUB + x, *parts)
+                return carry
+
+            lax.fori_loop(0, columns, widen_column, 0)
 
             def rims(at_start):
-                for side, (rim, prior) in enumerate(zip((west, east), before)):
+                for swap, (rim, prior) in enumerate(zip(halos, before)):
                     for c in range(SUB):
-                        at = c + side * (SUB + columns)
+                        at = c + (parity if swap else 1 - parity) * (SUB + columns)
                         if at_start:
                             end = prior.shape[2]
                             low = prior[level, c, end - 2 * MARGIN : end - MARGIN, :]
                             head = prior[level, c, end - MARGIN : end, :]
                             tail = rim[level, c, 0 : LANES - MARGIN, :]
                             if final:
-                                high = around[side][level, c, MARGIN : 2 * MARGIN, :]
+                                high = around[swap][level, c, MARGIN : 2 * MARGIN, :]
                             else:
                                 high = rim[level, c, LANES - MARGIN : LANES, :]
                         else:
@@ -323,20 +386,23 @@
                 pl.when(j == 0)(functools.partial(rims, True))
                 pl.when(j != 0)(functools.partial(rims, False))
 
-            for c in range(1, wide - 1):
-                both = jnp.dot(lhs, spread[c - 1], preferred_element_type=jnp.float32)
-                coef[2 * c - 2] = both[NEAR : top + NEAR, :LANES]
-                coef[2 * c - 1] = both[NEAR : top + NEAR, LANES:]
+            def substep_one(c, carry):
                 for r0, n in row_blocks(NEAR, LANES + 2 * NEAR, 72):
                     odd[c, r0 : r0 + n, :] = step(even, c, c - 1, r0, n)
-            for c in range(2, wide - 2):
+                return carry
+
+            def substep_two(c, carry):
                 for r0, n in row_blocks(NEAR, LANES + 2 * NEAR, 72):
                     even[c, r0 : r0 + n, :] = step(odd, c, c - 1, r0, n)
+                return carry
+
+            lax.fori_loop(1, wide - 1, substep_one, 0)
+            lax.fori_loop(2, wide - 2, substep_two, 0)
 
             for x in range(columns):
                 c = x + SUB
                 if level == 0:
-                    pair = jnp.dot(middle, spread[12 + x], preferred_element_type=jnp.float32)
+                    pair = jnp.dot(lhs[MARGIN:top], spread[12 + x], preferred_element_type=jnp.float32)
                     depth = pair[:, :LANES]
                     hot = jnp.where(pair[:, LANES:] == category, 1.0, 0.0).astype(jnp.bfloat16)
                     speed = jnp.dot(hot, speeds[...], preferred_element_type=jnp.float32)
@@ -350,16 +416,16 @@
                 projected = lax.dot_general(
                     table[...], rounded, (((1,), (1,)), ((), ())), preferred_element_type=jnp.float32
                 )
-                which = classes[block, x : x + 1, :]
+                which = classes[x : x + 1, :] if final else classes[block, x : x + 1, :]
                 dry = jnp.zeros((8, LANES), jnp.float32)
                 wet = jnp.zeros((8, LANES), jnp.float32)
                 for b in range(NBIN):
                     dry = jnp.where(which == b, projected[8 * b : 8 * b + 8], dry)
                     wet = jnp.where(which == b, projected[64 + 8 * b : 72 + 8 * b], wet)
                 at = 8 * level + x
-                moist = fields[block, MOIST_ROW + at : MOIST_ROW + at + 1, :]
-                thickness = fields[block, DEPTH_ROW + at : DEPTH_ROW + at + 1, :]
-                sun = fields[block, SUN_ROW + x : SUN_ROW + x + 1, :]
+                moist = field_row(block, MOIST_ROW + at)
+                thickness = field_row(block, DEPTH_ROW + at)
+                sun = field_row(block, SUN_ROW + x)
                 growth = moist / (1.0 - moist)
                 optical = (dry + growth * wet) * thickness
                 if level == 1:
@@ -411,23 +477,25 @@
     tile = thermal_anomaly.shape[1]
     gx, gy = lax.axis_size("gx"), lax.axis_size("gy")
     strips = ("gx", "gy")
-    up = [(i, i + 1) for i in range(gx * gy - 1)]
-    down = [(j, i) for i, j in up]
-    gx_up = [(i, i + 1) for i in range(gx - 1)]
-    gx_down = [(j, i) for i, j in gx_up]
+
+    def swaps(n):
+        pairs = [[(i, i + 1) for i in range(start, n - 1, 2)] for start in (0, 1)]
+        return [p + [(j, i) for i, j in p] for p in pairs]
+
     vmem = pl.BlockSpec(memory_space=pltpu.VMEM)
     smem = pl.BlockSpec(memory_space=pltpu.SMEM)
     hbm = pl.BlockSpec(memory_space=pltpu.HBM)
 
     mine = lax.axis_index("gy").astype(jnp.int32)
-    place = jnp.stack([mine, jnp.zeros((), jnp.int32)])
+    gx_odd = lax.rem(lax.axis_index("gx").astype(jnp.int32), 2)
+    place = jnp.stack([mine, jnp.zeros((), jnp.int32), gx_odd])
 
     def halo_shape(k):
         low, high = chunk_rows(k)
         return jax.ShapeDtypeStruct((levels, SUB, high - low, species), bf16)
 
     rim_shape = jax.ShapeDtypeStruct((2 * 8, LANES), f32)
-    *slices, rim_up, rim_down = pl.pallas_call(
+    *slices, rim_0, rim_1 = pl.pallas_call(
         first_slice_kernel,
         out_shape=(halo_shape(0), halo_shape(0), rim_shape, rim_shape),
         in_specs=[smem, hbm] + [vmem] * 3,
@@ -447,12 +515,11 @@
         name="slice_later",
     )(place, tracer_amounts)
 
-    from_low = lax.ppermute(rim_up, "gx", gx_up)
-    from_high = lax.ppermute(rim_down, "gx", gx_down)
-    wests, easts = [], []
+    rims = [lax.ppermute(r, "gx", p) for r, p in zip((rim_0, rim_1), swaps(gx))]
+    halos = []
     for k in range(len(CHUNKS)):
-        wests.append(lax.ppermute(slices[2 * k], strips, up))
-        easts.append(lax.ppermute(slices[2 * k + 1], strips, down))
+        pair = slices[2 * k : 2 * k + 2]
+        halos.append([lax.ppermute(h, strips, p) for h, p in zip(pair, swaps(gx * gy))])
 
     packed = pl.pallas_call(
         pack_kernel,
@@ -470,8 +537,7 @@
         stratum_depths,
         sun_elevation_factor,
         thermal_anomaly,
-        from_low,
-        from_high,
+        *rims,
     )
     fields = lax.all_to_all(packed, "gy", split_axis=0, concat_axis=0, tiled=True)
 
@@ -495,7 +561,23 @@
         scratch_shapes=[pltpu.VMEM((tile + 16, LANES), f32)],
         compiler_params=pltpu.CompilerParams(vmem_limit_bytes=4 * 1024 * 1024),
         name="warm",
-    )(place, thermal_anomaly, from_low, from_high, fields)
+    )(place, thermal_anomaly, *rims, fields)
+
+    whole = pl.pallas_call(
+        own_kernel,
+        out_shape=(
+            jax.ShapeDtypeStruct((levels, columns, LANES + 2 * MARGIN, species), bf16),
+            jax.ShapeDtypeStruct((FIELD_ROWS, LANES), f32),
+            jax.ShapeDtypeStruct((columns, LANES), jnp.int32),
+            jax.ShapeDtypeStruct((levels, LANES + 2 * MARGIN, LANES), bf16),
+        ),
+        in_specs=[smem, hbm] + [vmem] * 3,
+        out_specs=(vmem,) * 4,
+        scratch_shapes=[pltpu.SemaphoreType.DMA((3,))],
+        compiler_params=pltpu.CompilerParams(vmem_limit_bytes=4 * 1024 * 1024),
+        name="own",
+    )(place, tracer_amounts, fields, classes, turned)
+    own_inputs = [whole[1], whole[2], whole[3], whole[0]]
 
     spread = jnp.asarray(spread_matrix(), bf16)
     table = jnp.concatenate([arid_extinction_table, swelling_factors], axis=1).T
@@ -509,29 +591,19 @@
 
     def run_chunk(k, out, heat):
         first, final = k == 0, k == len(CHUNKS) - 1
-        operands = [
-            place,
-            arriving_irradiance,
-            fields,
-            classes,
-            turned,
-            spread,
-            table,
-            speeds,
-            tracer_amounts,
-            wests[k],
-            easts[k],
-        ]
+        operands = [place, arriving_irradiance, spread, table, speeds]
+        operands += own_inputs if final else [fields, classes, turned, tracer_amounts]
+        operands += halos[k]
         specs = [smem, smem] + [vmem] * 9
         heat_block = (levels * columns, LANES)
         out_shapes = [jax.ShapeDtypeStruct(tracer_amounts.shape, f32)]
         out_specs = [hbm]
         aliases = {}
         if not first:
-            operands += [wests[k - 1], easts[k - 1]]
+            operands += halos[k - 1]
             specs += [vmem] * 2
             if final:
-                operands += [wests[0], easts[0]]
+                operands += halos[0]
                 specs += [vmem] * 2
             aliases[len(operands)] = 0
             operands.append(out)

time: 149 us -> 146 us (0.980)
  the two profiles are of different devices: /device:TPU:18 before, /device:TPU:0 now
where the time goes in v2:
time: 146 us; the launch traced here: 144 us
  Pallas kernels  50.5 us (35%)
  waiting for transfers between devices  40 us (27%)
  starting transfers between devices  31.9 us (22%)
  local copies, waits for them, and re-layouts  17.9 us (12%)
  other arithmetic  2.84 us (2%)
    pallas_call x4, Pallas kernels, run_chunk(): pl.pallas_call(functools.partial(chunk_kernel, k), out_shape=tuple(out_sh...  44.2 us
    ppermute x8, waiting for transfers between devices, per_device(): lax.ppermute(h, strips, p)  28.6 us
    unnamed x62, local copies, waits for them, and re-layouts  17.8 us
    ppermute x8, starting transfers between devices, per_device(): lax.ppermute(h, strips, p)  12.9 us
    all_to_all x1, waiting for transfers between devices, per_device(): lax.all_to_all(packed, 'gy', split_axis=0, concat_axis=0, tiled=True)  11.2 us
    all_to_all x1, starting transfers between devices, per_device(): lax.all_to_all(packed, 'gy', split_axis=0, concat_axis=0, tiled=True)  7.41 us
    all_to_all x1, starting transfers between devices, per_device(): lax.all_to_all(heat, 'gy', split_axis=0, concat_axis=0, tiled=True)  6.11 us
    ppermute x2, starting transfers between devices, per_device(): rims = [lax.ppermute(r, 'gx', p) for r, p in zip((rim_0, rim_1), swaps(gx))]  5.49 us
  transfers between devices with their start and end apart: 12, of which 4 were waited for; matrix products, arithmetic and copies ran while one was open for 1% of the time, Pallas kernels for 34%

profile of v2, /device:TPU:0, one launch (start us, length us, event | category | flops | bytes accessed | tf_op | source)
XLA Modules:
  0.0 144.0 jit_solution(11281441380936276625)
XLA Ops:
  0.7 2.2 %copy-done = bf16[2,8,1024,128]{3,2,1,0:T(8,128)(2,1)S(1)} copy-done((bf16[2,8,1024,128]{3,2,1,0:T(8,128)(2,1)S(1)}, bf16[2,8,1024,128]{3,2,1,0:T(8,128)(2,1)}, u32[]{:S(2)}) %copy-start) | copy-done | bytes 4194328
  2.9 0.8 copy-done.7
  5.5 1.4 slice_first.1
  6.9 2.1 %collective-permute-start.6 = (bf16[2,3,288,128]{3,2,1,0:T(8,128)(2,1)}, bf16[2,3,288,128]{3,2,1,0:T(8,128)(2,1)S(1)}, u32[]{:S(2)}, u32[]{:S(2)}) collective-permute-start(bf16[2,3,288,128]{3,2,1,0:T(8,128)(2,1)} %get-tuple-element.38), channel_id=1, source_target_pairs={{0,1},{2,3},{4,5},{6,7},{8,9},{10,11},{12,13},{14,15},{16,17},{18,... | collective-permute-start | bytes 1327112 | tf_op jit(solution)/shard_map/ppermute | solution.py:522
  9.1 1.8 %slice_later.1 = (bf16[2,3,384,128]{3,2,1,0:T(8,128)(2,1)}, bf16[2,3,384,128]{3,2,1,0:T(8,128)(2,1)}, bf16[2,3,256,128]{3,2,1,0:T(8,128)(2,1)}, bf16[2,3,256,128...) custom-call(s32[3]{0:T(128)S(1)} %pad_add_fusion.place.refs_0_, ...), custom_call_target="tpu_custom_call" | custom-call | tf_op jit(solution)/shard_map/slice_later/pallas_call | solution.py:508
  13.1 1.5 %collective-permute-start.9 = (bf16[2,3,384,128]{3,2,1,0:T(8,128)(2,1)}, bf16[2,3,384,128]{3,2,1,0:T(8,128)(2,1)}, u32[]{:S(2)}, u32[]{:S(2)}) collective-permute-start(bf16[2,3,384,128]{3,2,1,0:T(8,128)(2,1)} %get-tuple-element.41), channel_id=1, source_target_pairs={{1,2},{3,4},{5,6},{7,8},{9,10},{11,12},{13,14},{15,16},{17,18},{19... | collective-permute-start | bytes 1769480 | tf_op jit(solution)/shard_map/ppermute | solution.py:522
  14.5 4.8 %collective-permute-start = (f32[16,128]{1,0:T(8,128)S(1)}, f32[16,128]{1,0:T(8,128)S(1)}, u32[]{:S(2)}, u32[]{:S(2)}) collective-permute-start(f32[16,128]{1,0:T(8,128)S(1)} %get-tuple-element.26), channel_id=1, source_target_pairs={{0,8},{16,24},{32,40},{48,56},{64,72},{80,88},{96,104},{112,120},{... | collective-permute-start | bytes 24584 | tf_op jit(solution)/shard_map/ppermute | solution.py:518
  20.9 2.3 %collective-permute-start.4 = (bf16[2,3,256,128]{3,2,1,0:T(8,128)(2,1)}, bf16[2,3,256,128]{3,2,1,0:T(8,128)(2,1)S(1)}, u32[]{:S(2)}, u32[]{:S(2)}) collective-permute-start(bf16[2,3,256,128]{3,2,1,0:T(8,128)(2,1)} %get-tuple-element.36), channel_id=1, source_target_pairs={{0,1},{2,3},{4,5},{6,7},{8,9},{10,11},{12,13},{14,15},{16,17},{18,... | collective-permute-start | bytes 1179656 | tf_op jit(solution)/shard_map/ppermute | solution.py:522
  23.2 1.4 pack.1
  25.2 7.4 %all-to-all-start = ((f32[8,96,128]{2,1,0:T(8,128)}), f32[8,96,128]{2,1,0:T(8,128)S(1)}, u32[]{:S(2)}, u32[]{:S(2)}) async-start(f32[8,96,128]{2,1,0:T(8,128)} %pack.1), calls=%async_computation | async-start | bytes 786432 | tf_op jit(solution)/shard_map/all_to_all | solution.py:542
  32.6 12.6 %collective-permute-done.6.refs_9_.refs_11_.refs_13_ = bf16[2,3,288,128]{3,2,1,0:T(8,128)(2,1)S(1)} collective-permute-done((bf16[2,3,288,128]{3,2,1,0:T(8,128)(2,1)}, bf16[2,3,288,128]{3,2,1,0:T(8,128)(2,1)S(1)}, u32[]{:S(2)}, u32[]{:S(2)}) %collective-permute-start.6) | collective-permute-done | bytes 442400 | tf_op jit(solution)/shard_map/ppermute | solution.py:522
  45.1 1.4 collective-permute-start.5
  46.8 3.6 %collective-permute-start.2 = (bf16[2,3,112,128]{3,2,1,0:T(8,128)(2,1)}, bf16[2,3,112,128]{3,2,1,0:T(8,128)(2,1)}, u32[]{:S(2)}, u32[]{:S(2)}) collective-permute-start(bf16[2,3,112,128]{3,2,1,0:T(8,128)(2,1)} %copy-done.26), channel_id=1, source_target_pairs={{0,1},{2,3},{4,5},{6,7},{8,9},{10,11},{12,13},{14,15},{16,17},{18,... | collective-permute-start | bytes 516104 | tf_op jit(solution)/shard_map/ppermute | solution.py:522
  50.4 16.0 %collective-permute-done.8.refs_9_.refs_11_ = bf16[2,3,384,128]{3,2,1,0:T(8,128)(2,1)} collective-permute-done((bf16[2,3,384,128]{3,2,1,0:T(8,128)(2,1)}, bf16[2,3,384,128]{3,2,1,0:T(8,128)(2,1)}, u32[]{:S(2)}, u32[]{:S(2)}) %collective-permute-start.8) | collective-permute-done | bytes 589856 | tf_op jit(solution)/shard_map/ppermute | solution.py:522
  66.4 1.3 collective-permute-start.3
  68.3 11.2 %all-to-all-done.fields.refs_5_ = f32[8,96,128]{2,1,0:T(8,128)S(1)} async-done(((f32[8,96,128]{2,1,0:T(8,128)}), f32[8,96,128]{2,1,0:T(8,128)S(1)}, u32[]{:S(2)}, u32[]{:S(2)}) %all-to-all-start) | async-done | bytes 393248 | tf_op jit(solution)/shard_map/all_to_all | solution.py:542
  81.3 2.2 %copy-done.1 = bf16[2,8,1024,128]{3,2,1,0:T(8,128)(2,1)S(1)} copy-done((bf16[2,8,1024,128]{3,2,1,0:T(8,128)(2,1)S(1)}, bf16[2,8,1024,128]{3,2,1,0:T(8,128)(2,1)}, u32[]{:S(2)}) %copy-start.1) | copy-done | bytes 4194328
  84.2 10.5 %shard_map.149 = (f32[2,8,1024,128]{3,2,1,0:T(8,128)}, f32[8,16,128]{2,1,0:T(8,128)S(1)}) custom-call(s32[3]{0:T(128)S(1)} %pad_add_fusion.place.refs_0_, f32[4]{0:T(128)S(1)} %copy-done.23, bf16[20,128,256]{2,1,0:T(8,128)(2,1)S(1)} %copy-done.3, bf16[128,128]{1,0:T(8,128)(2,1)S(1)} %copy-done.4, bf16[128,128]{1,0:T(8,128)(2,1)S(1)} %maximum_maximum_fusion.refs_4_, ...), custom_call_target="tpu_custom_call" | custom-call | flops 31457280 | bytes 4194304 | tf_op jit(solution)/shard_map/pallas_call | solution.py:623
  94.8 15.9 %shard_map.150 = (f32[2,8,1024,128]{3,2,1,0:T(8,128)}, f32[8,16,128]{2,1,0:T(8,128)S(1)}) custom-call(s32[3]{0:T(128)S(1)} %pad_add_fusion.place.refs_0_, f32[4]{0:T(128)S(1)} %copy-done.23, bf16[20,128,256]{2,1,0:T(8,128)(2,1)S(1)} %copy-done.3, bf16[128,128]{1,0:T(8,128)(2,1)S(1)} %copy-done.4, ...), custom_call_target="tpu_custom_call", output_to_operand_aliasing={{0}: (13, {}), {1}: (14, {})} | custom-call | flops 47185920 | bytes 6291456 | tf_op jit(solution)/shard_map/pallas_call | solution.py:623
  110.7 11.3 %shard_map.151 = (f32[2,8,1024,128]{3,2,1,0:T(8,128)}, f32[8,16,128]{2,1,0:T(8,128)S(1)}) custom-call(s32[3]{0:T(128)S(1)} %pad_add_fusion.place.refs_0_, f32[4]{0:T(128)S(1)} %copy-done.23, bf16[20,128,256]{2,1,0:T(8,128)(2,1)S(1)} %copy-done.3, bf16[128,128]{1,0:T(8,128)(2,1)S(1)} %copy-done.4, ...), custom_call_target="tpu_custom_call", output_to_operand_aliasing={{0}: (13, {}), {1}: (14, {})} | custom-call | flops 31457280 | bytes 4194304 | tf_op jit(solution)/shard_map/pallas_call | solution.py:623
  122.7 6.1 %all-to-all-start.1 = ((f32[8,16,128]{2,1,0:T(8,128)}), f32[8,16,128]{2,1,0:T(8,128)}, u32[]{:S(2)}, u32[]{:S(2)}) async-start(f32[8,16,128]{2,1,0:T(8,128)} %copy-done.6), calls=%async_computation.1 | async-start | bytes 131072 | tf_op jit(solution)/shard_map/all_to_all | solution.py:648
  129.3 2.2 %copy-done.2 = bf16[2,8,1024,128]{3,2,1,0:T(8,128)(2,1)S(1)} copy-done((bf16[2,8,1024,128]{3,2,1,0:T(8,128)(2,1)S(1)}, bf16[2,8,1024,128]{3,2,1,0:T(8,128)(2,1)}, u32[]{:S(2)}) %copy-start.2) | copy-done | bytes 4194328
  136.0 6.5 %shard_map.152 = (f32[2,8,1024,128]{3,2,1,0:T(8,128)}, f32[16,128]{1,0:T(8,128)S(1)}) custom-call(s32[3]{0:T(128)S(1)} %pad_add_fusion.place.refs_0_, f32[4]{0:T(128)S(1)} %copy-done.23, bf16[20,128,256]{2,1,0:T(8,128)(2,1)S(1)} %copy-done.3, bf16[128,128]{1,0:T(8,128)(2,1)S(1)} %copy-done.5, ...), custom_call_target="tpu_custom_call", output_to_operand_aliasing={{0}: (15, {})} | custom-call | flops 15728640 | bytes 2097152 | tf_op jit(solution)/shard_map/pallas_call | solution.py:623
  142.5 1.5 %bitcast_add_fusion = f32[2,64,128]{2,1,0:T(8,128)} fusion(f32[2,64,128]{2,1,0:T(8,128)S(1)} %warm.1, f32[8,16,128]{2,1,0:T(8,128)} %all-to-all-done.1, f32[16,128]{1,0:T(8,128)S(1)} %get-tuple-element.48, pred[8]{0:T(512)(128)(4,1)S(1)} %copy-done.30), kind=kLoop, calls=%fused_computation | loop fusion | flops 32768 | bytes 204808 | tf_op jit(solution)/shard_map/add | solution.py:654
  (80 shorter events, 14.9 us)
Async XLA Ops:
  0.6 45.9 %copy-start.29 = (f32[24,128]{1,0:T(8,128)S(1)}, f32[24,128]{1,0:T(8,128)}, u32[]{:S(2)}) copy-start(f32[24,128]{1,0:T(8,128)} %param.25) | copy-start | bytes 36868
  0.6 67.1 %copy-start.27 = (bf16[128,64]{0,1:T(8,128)(2,1)S(1)}, bf16[128,64]{0,1:T(8,128)(2,1)}, u32[]{:S(2)}) copy-start(bf16[128,64]{0,1:T(8,128)(2,1)} %param.24) | copy-start | bytes 49156
  0.7 80.6 %copy-start.23 = (f32[4]{0:T(128)S(1)}, f32[4]{0:T(128)}, u32[]{:S(2)}) copy-start(f32[4]{0:T(128)} %refs_1_.7) | copy-start | bytes 52
  5.5 17.7 %copy-start.8 = (f32[2,64,128]{2,1,0:T(8,128)S(1)}, f32[2,64,128]{2,1,0:T(8,128)}, u32[]{:S(2)}) copy-start(f32[2,64,128]{2,1,0:T(8,128)} %warmth.5) | copy-start | bytes 196612
  5.5 17.7 %copy-start.13 = (f32[2,64,128]{2,1,0:T(8,128)S(1)}, f32[2,64,128]{2,1,0:T(8,128)}, u32[]{:S(2)}) copy-start(f32[2,64,128]{2,1,0:T(8,128)} %u.3) | copy-start | bytes 196612
  5.5 17.7 %copy-start.15 = (f32[2,64,128]{2,1,0:T(8,128)S(1)}, f32[2,64,128]{2,1,0:T(8,128)}, u32[]{:S(2)}) copy-start(f32[2,64,128]{2,1,0:T(8,128)} %v.3) | copy-start | bytes 196612
  5.5 17.7 %copy-start.16 = (f32[2,64,128]{2,1,0:T(8,128)S(1)}, f32[2,64,128]{2,1,0:T(8,128)}, u32[]{:S(2)}) copy-start(f32[2,64,128]{2,1,0:T(8,128)} %moisture.1) | copy-start | bytes 196612
  5.5 17.7 %copy-start.17 = (f32[2,64,128]{2,1,0:T(8,128)S(1)}, f32[2,64,128]{2,1,0:T(8,128)}, u32[]{:S(2)}) copy-start(f32[2,64,128]{2,1,0:T(8,128)} %depth.1) | copy-start | bytes 196612
  5.5 17.7 %copy-start.22 = (f32[64,128]{1,0:T(8,128)S(1)}, f32[64,128]{1,0:T(8,128)}, u32[]{:S(2)}) copy-start(f32[64,128]{1,0:T(8,128)} %sun.1) | copy-start | bytes 98308
  5.5 62.2 %copy-start.28 = (bf16[128,64]{0,1:T(8,128)(2,1)S(1)}, bf16[128,64]{0,1:T(8,128)(2,1)}, u32[]{:S(2)}) copy-start(bf16[128,64]{0,1:T(8,128)(2,1)} %param.23) | copy-start | bytes 49156
  5.5 75.8 %copy-start.3 = (bf16[20,128,256]{2,1,0:T(8,128)(2,1)S(1)}, bf16[20,128,256]{2,1,0:T(8,128)(2,1)}, u32[]{:S(2)}) copy-start(bf16[20,128,256]{2,1,0:T(8,128)(2,1)} %constant.20.clone.refs_2_) | copy-start | bytes 3932164
  6.9 38.2 %collective-permute-start.6 = (bf16[2,3,288,128]{3,2,1,0:T(8,128)(2,1)}, bf16[2,3,288,128]{3,2,1,0:T(8,128)(2,1)S(1)}, u32[]{:S(2)}, u32[]{:S(2)}) collective-permute-start(bf16[2,3,288,128]{3,2,1,0:T(8,128)(2,1)} %get-tuple-element.38), channel_id=1, source_target_pairs={{0,1},{2,3},{4,5},{6,7},{8,9},{10,11},{12,13},{14,15},{16,17},{18,... | collective-permute-start | bytes 1327112 | tf_op jit(solution)/shard_map/ppermute | solution.py:522
  13.0 53.3 %collective-permute-start.8 = (bf16[2,3,384,128]{3,2,1,0:T(8,128)(2,1)}, bf16[2,3,384,128]{3,2,1,0:T(8,128)(2,1)}, u32[]{:S(2)}, u32[]{:S(2)}) collective-permute-start(bf16[2,3,384,128]{3,2,1,0:T(8,128)(2,1)} %get-tuple-element.40), channel_id=1, source_target_pairs={{0,1},{2,3},{4,5},{6,7},{8,9},{10,11},{12,13},{14,15},{16,17},{18,... | collective-permute-start | bytes 1769480 | tf_op jit(solution)/shard_map/ppermute | solution.py:522
  13.1 81.7 %collective-permute-start.9 = (bf16[2,3,384,128]{3,2,1,0:T(8,128)(2,1)}, bf16[2,3,384,128]{3,2,1,0:T(8,128)(2,1)}, u32[]{:S(2)}, u32[]{:S(2)}) collective-permute-start(bf16[2,3,384,128]{3,2,1,0:T(8,128)(2,1)} %get-tuple-element.41), channel_id=1, source_target_pairs={{1,2},{3,4},{5,6},{7,8},{9,10},{11,12},{13,14},{15,16},{17,18},{19... | collective-permute-start | bytes 1769480 | tf_op jit(solution)/shard_map/ppermute | solution.py:522
  14.5 5.7 %collective-permute-start = (f32[16,128]{1,0:T(8,128)S(1)}, f32[16,128]{1,0:T(8,128)S(1)}, u32[]{:S(2)}, u32[]{:S(2)}) collective-permute-start(f32[16,128]{1,0:T(8,128)S(1)} %get-tuple-element.26), channel_id=1, source_target_pairs={{0,8},{16,24},{32,40},{48,56},{64,72},{80,88},{96,104},{112,120},{... | collective-permute-start | bytes 24584 | tf_op jit(solution)/shard_map/ppermute | solution.py:518
  19.4 1.5 %collective-permute-start.1 = (f32[16,128]{1,0:T(8,128)S(1)}, f32[16,128]{1,0:T(8,128)S(1)}, u32[]{:S(2)}, u32[]{:S(2)}) collective-permute-start(f32[16,128]{1,0:T(8,128)S(1)} %get-tuple-element.27), channel_id=1, source_target_pairs={{8,16},{24,32},{40,48},{56,64},{72,80},{88,96},{104,112},{16,8},{3... | collective-permute-start | bytes 24584 | tf_op jit(solution)/shard_map/ppermute | solution.py:518
  20.2 26.6 %collective-permute-start.7 = (bf16[2,3,288,128]{3,2,1,0:T(8,128)(2,1)S(1)}, bf16[2,3,288,128]{3,2,1,0:T(8,128)(2,1)S(1)}, u32[]{:S(2)}, u32[]{:S(2)}) collective-permute-start(bf16[2,3,288,128]{3,2,1,0:T(8,128)(2,1)S(1)} %get-tuple-element.39), channel_id=1, source_target_pairs={{1,2},{3,4},{5,6},{7,8},{9,10},{11,12},{13,14},{15,16},{17,18},{19... | collective-permute-start | bytes 1327112 | tf_op jit(solution)/shard_map/ppermute | solution.py:522
  20.9 89.8 %collective-permute-start.4 = (bf16[2,3,256,128]{3,2,1,0:T(8,128)(2,1)}, bf16[2,3,256,128]{3,2,1,0:T(8,128)(2,1)S(1)}, u32[]{:S(2)}, u32[]{:S(2)}) collective-permute-start(bf16[2,3,256,128]{3,2,1,0:T(8,128)(2,1)} %get-tuple-element.36), channel_id=1, source_target_pairs={{0,1},{2,3},{4,5},{6,7},{8,9},{10,11},{12,13},{14,15},{16,17},{18,... | collective-permute-start | bytes 1179656 | tf_op jit(solution)/shard_map/ppermute | solution.py:522
  25.2 54.4 %all-to-all-start = ((f32[8,96,128]{2,1,0:T(8,128)}), f32[8,96,128]{2,1,0:T(8,128)S(1)}, u32[]{:S(2)}, u32[]{:S(2)}) async-start(f32[8,96,128]{2,1,0:T(8,128)} %pack.1), calls=%async_computation | async-start | bytes 786432 | tf_op jit(solution)/shard_map/all_to_all | solution.py:542
  45.1 65.5 %collective-permute-start.5 = (bf16[2,3,256,128]{3,2,1,0:T(8,128)(2,1)}, bf16[2,3,256,128]{3,2,1,0:T(8,128)(2,1)}, u32[]{:S(2)}, u32[]{:S(2)}) collective-permute-start(bf16[2,3,256,128]{3,2,1,0:T(8,128)(2,1)} %copy-done.24), channel_id=1, source_target_pairs={{1,2},{3,4},{5,6},{7,8},{9,10},{11,12},{13,14},{15,16},{17,18},{19... | collective-permute-start | bytes 1179656 | tf_op jit(solution)/shard_map/ppermute | solution.py:522
  46.8 88.5 %collective-permute-start.2 = (bf16[2,3,112,128]{3,2,1,0:T(8,128)(2,1)}, bf16[2,3,112,128]{3,2,1,0:T(8,128)(2,1)}, u32[]{:S(2)}, u32[]{:S(2)}) collective-permute-start(bf16[2,3,112,128]{3,2,1,0:T(8,128)(2,1)} %copy-done.26), channel_id=1, source_target_pairs={{0,1},{2,3},{4,5},{6,7},{8,9},{10,11},{12,13},{14,15},{16,17},{18,... | collective-permute-start | bytes 516104 | tf_op jit(solution)/shard_map/ppermute | solution.py:522
  66.4 68.9 %collective-permute-start.3 = (bf16[2,3,112,128]{3,2,1,0:T(8,128)(2,1)}, bf16[2,3,112,128]{3,2,1,0:T(8,128)(2,1)}, u32[]{:S(2)}, u32[]{:S(2)}) collective-permute-start(bf16[2,3,112,128]{3,2,1,0:T(8,128)(2,1)} %copy-done.25), channel_id=1, source_target_pairs={{1,2},{3,4},{5,6},{7,8},{9,10},{11,12},{13,14},{15,16},{17,18},{19... | collective-permute-start | bytes 516104 | tf_op jit(solution)/shard_map/ppermute | solution.py:522
  81.3 29.4 %copy-start.10 = (s32[8,8,128]{2,1,0:T(8,128)}, s32[8,8,128]{2,1,0:T(8,128)S(1)}, u32[]{:S(2)}) copy-start(s32[8,8,128]{2,1,0:T(8,128)S(1)} %get-tuple-element.28.classes.refs_6_) | copy-start | bytes 98308
  122.7 19.8 %all-to-all-start.1 = ((f32[8,16,128]{2,1,0:T(8,128)}), f32[8,16,128]{2,1,0:T(8,128)}, u32[]{:S(2)}, u32[]{:S(2)}) async-start(f32[8,16,128]{2,1,0:T(8,128)} %copy-done.6), calls=%async_computation.1 | async-start | bytes 131072 | tf_op jit(solution)/shard_map/all_to_all | solution.py:648
  (19 other events, 25.8 us)

commit v3 on v2

--- a/solution.py
+++ b/solution.py
@@ -18,7 +18,7 @@
 MARGIN = 16
 NEAR = 8
 RIM = 2
-CHUNKS = (2, 3, 2, 1)
+CHUNKS = (1, 3, 2, 1, 1)
 
 UV_ROWS = 24
 MOIST_ROW = 48
@@ -27,6 +27,8 @@
 EDGE_ROW = 88
 FIELD_ROWS = 96
 PAIRS = 20
+SPAN = LANES + 2 * MARGIN
+COEF_SPAN = LANES + 2 * NEAR
 
 
 def spread_matrix():
@@ -40,6 +42,10 @@
             out[12 + x, 72 + 8 * part + x, :LANES] = 1.0
         out[12 + x, 96 + x, LANES:] = 1.0
     return out
+
+
+def hold(*arrays):
+    return [pltpu.with_memory_space_constraint(x, pltpu.HBM) for x in arrays]
 
 
 def three_parts(x):
@@ -115,8 +121,15 @@
 
 
 def later_slice_kernel(place, tracer, *refs):
-    outs, sems = refs[:-1], refs[-1]
-    copies = slice_copies(tuple(range(1, len(CHUNKS))), place, tracer, outs, sems)
+    later = tuple(range(1, len(CHUNKS)))
+    n = 2 * len(later)
+    outs, stages, sems, out_sems = refs[:n], refs[n : 2 * n], refs[2 * n], refs[2 * n + 1]
+    copies = slice_copies(later, place, tracer, stages, sems)
+    for copy in copies:
+        copy.start()
+    for copy in copies:
+        copy.wait()
+    copies = [pltpu.make_async_copy(stages[i], outs[i], out_sems.at[i]) for i in range(n)]
     for copy in copies:
         copy.start()
     for copy in copies:
@@ -196,31 +209,6 @@
         out[level] = here + SPREAD_FACTOR * laplace
 
 
-def own_kernel(place, tracer, fields, classes, turned, window, own_fields, own_classes, lhs, sems):
-    mine = place[0]
-    blocks = fields.shape[0]
-    row = pl.multiple_of(mine * LANES, LANES)
-    low = pl.multiple_of(jnp.maximum(row - MARGIN, 0), MARGIN)
-    high = pl.multiple_of(jnp.minimum(row + LANES, tracer.shape[2] - MARGIN), MARGIN)
-    copies = []
-    for source, at, n in ((low, 0, MARGIN), (row, MARGIN, LANES), (high, MARGIN + LANES, MARGIN)):
-        copies.append(
-            pltpu.make_async_copy(
-                tracer.at[:, :, pl.ds(source, n), :],
-                window.at[:, :, at : at + n, :],
-                sems.at[len(copies)],
-            )
-        )
-    for copy in copies:
-        copy.start()
-    own_fields[...] = fields[mine]
-    own_classes[...] = classes[mine]
-    for level in range(2):
-        lhs[level] = block_lhs(turned, level, mine, blocks)
-    for copy in copies:
-        copy.wait()
-
-
 def block_lhs(turned, level, block, blocks):
     low = turned[level, jnp.maximum(block - 1, 0), LANES - MARGIN :, :].astype(jnp.float32)
     high = turned[level, jnp.minimum(block + 1, blocks - 1), :MARGIN, :].astype(jnp.float32)
@@ -230,6 +218,50 @@
     return jnp.concatenate([ends[0], turned[level, block], ends[1]], axis=0)
 
 
+def coefficient_kernel(turned, spread, speeds, coef, share, stage, hot, kept, sems, share_sem):
+    blocks = coef.shape[0]
+    lane = lax.broadcasted_iota(jnp.int32, (1, LANES), 1)
+    category = jnp.where(lane < 72, lane % 24, -1).astype(jnp.float32)
+    columns = share.shape[1]
+
+    def copies(block, level):
+        these = [pltpu.make_async_copy(stage.at[level], coef.at[block, level], sems.at[level])]
+        if level == 0:
+            these.append(pltpu.make_async_copy(kept, share.at[block], share_sem.at[0]))
+        return these
+
+    def one_block(block, carry):
+        for level in (1, 0):
+
+            @pl.when(block > 0)
+            def _():
+                for copy in copies(block - 1, level):
+                    copy.wait()
+
+            lhs = block_lhs(turned, level, block, blocks)
+            for c in range(stage.shape[1] // 2):
+                both = jnp.dot(lhs, spread[c], preferred_element_type=jnp.float32)
+                stage[level, 2 * c] = both[NEAR : NEAR + COEF_SPAN, :LANES]
+                stage[level, 2 * c + 1] = both[NEAR : NEAR + COEF_SPAN, LANES:]
+            if level == 0:
+                middle = lhs[MARGIN : MARGIN + LANES]
+                for x in range(columns):
+                    pair = jnp.dot(middle, spread[12 + x], preferred_element_type=jnp.float32)
+                    kept[x] = pair[:, :LANES]
+                    hot[x] = jnp.where(pair[:, LANES:] == category, 1.0, 0.0).astype(jnp.bfloat16)
+                for x in range(columns):
+                    speed = jnp.dot(hot[x], speeds[...], preferred_element_type=jnp.float32)
+                    kept[x] = kept[x] / (kept[x] + speed)
+            for copy in copies(block, level):
+                copy.start()
+        return carry
+
+    lax.fori_loop(0, blocks, one_block, 0)
+    for level in (1, 0):
+        for copy in copies(blocks - 1, level):
+            copy.wait()
+
+
 def row_blocks(first, count, size):
     return [(r, min(size, first + count - r)) for r in range(first, first + count, size)]
 
@@ -238,8 +270,8 @@
     first, final = k == 0, k == len(CHUNKS) - 1
     count = CHUNKS[k]
     refs = list(refs)
-    place, sunlight, spread, table, speeds, fields, classes, turned, tracer = refs[:9]
-    del refs[:9]
+    place, sunlight, table, fields, classes, tracer, all_coef, all_share = refs[:8]
+    del refs[:8]
     halos = refs[:2]
     del refs[:2]
     before = (None, None)
@@ -254,7 +286,8 @@
         else:
             del refs[:2]
     out, heat = refs[:2]
-    even, odd, coef, result, thick, warm, out_sems, heat_sems = refs[2:]
+    window, even, odd, coef, kept, result, thick, warm = refs[2:10]
+    in_sems, coef_sems, out_sems, heat_sems = refs[10:]
 
     columns = 8
     wide = columns + 2 * SUB
@@ -268,11 +301,39 @@
     weights = jnp.zeros((8, LANES), jnp.float32)
     for w in range(NW):
         weights = jnp.where(sublane == NW + w, sunlight[w], weights)
-    lane = lax.broadcasted_iota(jnp.int32, (1, LANES), 1)
-    category = jnp.where(lane < 72, lane % 24, -1).astype(jnp.float32)
 
     def wide_of(x):
         return x.astype(jnp.float32)
+
+    def loads(j, slot, level):
+        block = lax.rem(mine + 1 + sum(CHUNKS[:k]) + j, blocks)
+        row = pl.multiple_of(block * LANES, LANES)
+        low = pl.multiple_of(jnp.maximum(row - MARGIN, 0), MARGIN)
+        high = pl.multiple_of(jnp.minimum(row + LANES, grid_rows - MARGIN), MARGIN)
+        return [
+            pltpu.make_async_copy(
+                tracer.at[level, :, pl.ds(at, n), :],
+                window.at[slot, level, :, to : to + n, :],
+                in_sems.at[slot, level, i],
+            )
+            for i, (at, to, n) in enumerate(
+                ((low, 0, MARGIN), (row, MARGIN, LANES), (high, MARGIN + LANES, MARGIN))
+            )
+        ]
+
+    def load_block(j, slot):
+        for level in (1, 0):
+            for copy in loads(j, slot, level):
+                copy.start()
+
+    def coef_loads(j, level):
+        block = lax.rem(mine + 1 + sum(CHUNKS[:k]) + j, blocks)
+        these = [
+            pltpu.make_async_copy(all_coef.at[block, level], coef.at[level], coef_sems.at[level])
+        ]
+        if level == 0:
+            these.append(pltpu.make_async_copy(all_share.at[block], kept, coef_sems.at[2]))
+        return these
 
     def copies(j, slot, which=None):
         block = lax.rem(mine + 1 + sum(CHUNKS[:k]) + j, blocks)
@@ -287,12 +348,12 @@
         return these
 
     def field_row(block, at):
-        return fields[at : at + 1, :] if final else fields[block, at : at + 1, :]
-
-    def step(source, c, i, r0, n):
+        return fields[block, at : at + 1, :]
+
+    def step(level, source, c, i, r0, n):
         here = source[c, r0 : r0 + n, :]
-        u = coef[2 * i, r0 - NEAR : r0 - NEAR + n, :]
-        v = coef[2 * i + 1, r0 - NEAR : r0 - NEAR + n, :]
+        u = coef[level, 2 * i, r0 - NEAR : r0 - NEAR + n, :]
+        v = coef[level, 2 * i + 1, r0 - NEAR : r0 - NEAR + n, :]
         across = jnp.where(u > 0.0, source[c - 1, r0 : r0 + n, :], source[c + 1, r0 : r0 + n, :])
         along = jnp.where(
             v > 0.0, source[c, pl.ds(z + (r0 - 1), n), :], source[c, pl.ds(z + (r0 + 1), n), :]
@@ -302,11 +363,14 @@
     def one_block(j, carry):
         slot = lax.rem(j, 2)
         block = lax.rem(mine + 1 + sum(CHUNKS[:k]) + j, blocks)
-        row = pl.multiple_of(block * LANES, LANES)
-        low_row = pl.multiple_of(jnp.maximum(row - MARGIN, 0), MARGIN)
-        high_row = pl.multiple_of(jnp.minimum(row + LANES, grid_rows - MARGIN), MARGIN)
         has_low = jnp.where(block != 0, 1.0, 0.0)
         has_high = jnp.where(block != blocks - 1, 1.0, 0.0)
+
+        if count > 1:
+
+            @pl.when(j + 1 < count)
+            def _():
+                load_block(j + 1, 1 - slot)
 
         if count > 2:
 
@@ -316,37 +380,25 @@
                     copy.wait()
 
         for level in (1, 0):
-            lhs = turned[level] if final else block_lhs(turned, level, block, blocks)
-            for c in range(wide - 2):
-                both = jnp.dot(lhs, spread[c], preferred_element_type=jnp.float32)
-                coef[2 * c] = both[NEAR : top + NEAR, :LANES]
-                coef[2 * c + 1] = both[NEAR : top + NEAR, LANES:]
-
             def widen(at, low, head, tail, high):
                 even[at, NEAR:MARGIN, :] = wide_of(low)[NEAR:, :] * has_low
                 even[at, MARGIN : 2 * MARGIN, :] = wide_of(head)
                 even[at, 2 * MARGIN : top, :] = wide_of(tail)
                 even[at, top : top + NEAR, :] = wide_of(high)[:NEAR, :] * has_high
 
+            for copy in loads(j, slot, level):
+                copy.wait()
+
             def widen_column(x, carry):
-                if final:
-                    parts = [
-                        tracer[level, x, r : r + n, :]
-                        for r, n in (
-                            (0, MARGIN),
-                            (MARGIN, MARGIN),
-                            (2 * MARGIN, LANES - MARGIN),
-                            (top, MARGIN),
-                        )
-                    ]
-                else:
-                    inner = pl.multiple_of(row + MARGIN, MARGIN)
-                    parts = [
-                        tracer[level, x, pl.ds(low_row, MARGIN), :],
-                        tracer[level, x, pl.ds(row, MARGIN), :],
-                        tracer[level, x, pl.ds(inner, LANES - MARGIN), :],
-                        tracer[level, x, pl.ds(high_row, MARGIN), :],
-                    ]
+                parts = [
+                    window[slot, level, x, r : r + n, :]
+                    for r, n in (
+                        (0, MARGIN),
+                        (MARGIN, MARGIN),
+                        (2 * MARGIN, LANES - MARGIN),
+                        (top, MARGIN),
+                    )
+                ]
                 widen(SUB + x, *parts)
                 return carry
 
@@ -388,35 +440,43 @@
 
             def substep_one(c, carry):
                 for r0, n in row_blocks(NEAR, LANES + 2 * NEAR, 72):
-                    odd[c, r0 : r0 + n, :] = step(even, c, c - 1, r0, n)
+                    odd[c, r0 : r0 + n, :] = step(level, even, c, c - 1, r0, n)
                 return carry
 
             def substep_two(c, carry):
                 for r0, n in row_blocks(NEAR, LANES + 2 * NEAR, 72):
-                    even[c, r0 : r0 + n, :] = step(odd, c, c - 1, r0, n)
+                    even[c, r0 : r0 + n, :] = step(level, odd, c, c - 1, r0, n)
                 return carry
 
+            for copy in coef_loads(j, level):
+                copy.wait()
             lax.fori_loop(1, wide - 1, substep_one, 0)
             lax.fori_loop(2, wide - 2, substep_two, 0)
 
+            def substep_three(x, carry):
+                c = x + SUB
+                for r0, n in row_blocks(MARGIN, LANES, 64):
+                    now = step(level, even, c, c - 1, r0, n)
+                    if level == 0:
+                        now = now * kept[x, r0 - MARGIN : r0 - MARGIN + n, :]
+                    result[slot, level, x, r0 - MARGIN : r0 - MARGIN + n, :] = now
+                return carry
+
+            lax.fori_loop(0, columns, substep_three, 0)
+            copies(j, slot, level)[0].start()
+            if count > 1:
+
+                @pl.when(j + 1 < count)
+                def _():
+                    for copy in coef_loads(j + 1, level):
+                        copy.start()
+
             for x in range(columns):
-                c = x + SUB
-                if level == 0:
-                    pair = jnp.dot(lhs[MARGIN:top], spread[12 + x], preferred_element_type=jnp.float32)
-                    depth = pair[:, :LANES]
-                    hot = jnp.where(pair[:, LANES:] == category, 1.0, 0.0).astype(jnp.bfloat16)
-                    speed = jnp.dot(hot, speeds[...], preferred_element_type=jnp.float32)
-                for r0, n in row_blocks(MARGIN, LANES, 64):
-                    now = step(even, c, c - 1, r0, n)
-                    if level == 0:
-                        part = slice(r0 - MARGIN, r0 - MARGIN + n)
-                        now = now * depth[part] / (depth[part] + speed[part])
-                    result[slot, level, x, r0 - MARGIN : r0 - MARGIN + n, :] = now
                 rounded = result[slot, level, x].astype(jnp.bfloat16)
                 projected = lax.dot_general(
                     table[...], rounded, (((1,), (1,)), ((), ())), preferred_element_type=jnp.float32
                 )
-                which = classes[x : x + 1, :] if final else classes[block, x : x + 1, :]
+                which = classes[block, x : x + 1, :]
                 dry = jnp.zeros((8, LANES), jnp.float32)
                 wet = jnp.zeros((8, LANES), jnp.float32)
                 for b in range(NBIN):
@@ -439,11 +499,14 @@
                     heat[at : at + 1, :] = lit
                 else:
                     warm[slot, at : at + 1, :] = lit
-            copies(j, slot, level)[0].start()
         if not final:
             copies(j, slot, 2)[0].start()
         return carry
 
+    load_block(0, 0)
+    for level in (1, 0):
+        for copy in coef_loads(0, level):
+            copy.start()
     if count == 1:
         one_block(0, 0)
     else:
@@ -455,6 +518,58 @@
         copy = pltpu.make_async_copy(warm.at[0], heat.at[mine], heat_sems.at[0])
         copy.start()
         copy.wait()
+
+
+def chunk_call(k, operands, out, heat, shape, gy):
+    first, final = k == 0, k == len(CHUNKS) - 1
+    levels, columns, _, _ = shape
+    vmem = pl.BlockSpec(memory_space=pltpu.VMEM)
+    smem = pl.BlockSpec(memory_space=pltpu.SMEM)
+    hbm = pl.BlockSpec(memory_space=pltpu.HBM)
+    operands = list(operands)
+    specs = [smem, smem] + [vmem] * 3 + [hbm] * 3 + [vmem] * (len(operands) - 8)
+    heat_block = (levels * columns, LANES)
+    out_shapes = [jax.ShapeDtypeStruct(shape, jnp.float32)]
+    out_specs = [hbm]
+    aliases = {}
+    if not first:
+        aliases[len(operands)] = 0
+        operands.append(out)
+        specs.append(hbm)
+    if final:
+        out_shapes.append(jax.ShapeDtypeStruct(heat_block, jnp.float32))
+        out_specs.append(vmem)
+    else:
+        if not first:
+            aliases[len(operands)] = 1
+            operands.append(heat)
+            specs.append(hbm)
+        out_shapes.append(jax.ShapeDtypeStruct((gy,) + heat_block, jnp.float32))
+        out_specs.append(hbm)
+    work = CHUNKS[k] * LANES * columns * levels * LANES
+    return pl.pallas_call(
+        functools.partial(chunk_kernel, k),
+        out_shape=tuple(out_shapes),
+        in_specs=specs,
+        out_specs=tuple(out_specs),
+        scratch_shapes=[
+            pltpu.VMEM((2, levels, columns, SPAN, LANES), jnp.bfloat16),
+            pltpu.VMEM((columns + 2 * SUB, SPAN, LANES), jnp.float32),
+            pltpu.VMEM((columns + 2 * SUB, SPAN, LANES), jnp.float32),
+            pltpu.VMEM((levels, 24, COEF_SPAN, LANES), jnp.float32),
+            pltpu.VMEM((columns, LANES, LANES), jnp.float32),
+            pltpu.VMEM((2, levels, columns, LANES, LANES), jnp.float32),
+            pltpu.VMEM((columns, 8, LANES), jnp.float32),
+            pltpu.VMEM((2, levels * columns, LANES), jnp.float32),
+            pltpu.SemaphoreType.DMA((2, levels, 3)),
+            pltpu.SemaphoreType.DMA((3,)),
+            pltpu.SemaphoreType.DMA((2, levels)),
+            pltpu.SemaphoreType.DMA((2,)),
+        ],
+        input_output_aliases=aliases,
+        compiler_params=pltpu.CompilerParams(vmem_limit_bytes=12 * 1024 * 1024),
+        cost_estimate=pl.CostEstimate(flops=60 * work, transcendentals=0, bytes_accessed=8 * work),
+    )(*operands)
 
 
 def per_device(
@@ -499,21 +614,31 @@
         first_slice_kernel,
         out_shape=(halo_shape(0), halo_shape(0), rim_shape, rim_shape),
         in_specs=[smem, hbm] + [vmem] * 3,
-        out_specs=(hbm, hbm, vmem, vmem),
+        out_specs=(vmem,) * 4,
         scratch_shapes=[pltpu.SemaphoreType.DMA((copy_count((0,)),))],
         compiler_params=pltpu.CompilerParams(vmem_limit_bytes=4 * 1024 * 1024),
         name="slice_first",
-    )(place, tracer_amounts, zonal_transit_ratio, meridional_transit_ratio, thermal_anomaly)
+    )(
+        place,
+        *hold(tracer_amounts, zonal_transit_ratio, meridional_transit_ratio, thermal_anomaly),
+    )
     later = tuple(range(1, len(CHUNKS)))
-    slices += pl.pallas_call(
-        later_slice_kernel,
-        out_shape=tuple(halo_shape(k) for k in later for _ in range(2)),
-        in_specs=[smem, hbm],
-        out_specs=(hbm,) * (2 * len(later)),
-        scratch_shapes=[pltpu.SemaphoreType.DMA((copy_count(later),))],
-        compiler_params=pltpu.CompilerParams(vmem_limit_bytes=4 * 1024 * 1024),
-        name="slice_later",
-    )(place, tracer_amounts)
+    later_shapes = [halo_shape(k) for k in later for _ in range(2)]
+    slices += hold(
+        *pl.pallas_call(
+            later_slice_kernel,
+            out_shape=tuple(pltpu.HBM(x.shape, x.dtype) for x in later_shapes),
+            in_specs=[smem, hbm],
+            out_specs=(hbm,) * len(later_shapes),
+            scratch_shapes=[pltpu.VMEM(x.shape, x.dtype) for x in later_shapes]
+            + [
+                pltpu.SemaphoreType.DMA((copy_count(later),)),
+                pltpu.SemaphoreType.DMA((len(later_shapes),)),
+            ],
+            compiler_params=pltpu.CompilerParams(vmem_limit_bytes=8 * 1024 * 1024),
+            name="slice_later",
+        )(place, *hold(tracer_amounts))
+    )
 
     rims = [lax.ppermute(r, "gx", p) for r, p in zip((rim_0, rim_1), swaps(gx))]
     halos = []
@@ -531,12 +656,14 @@
         name="pack",
     )(
         place,
-        zonal_transit_ratio,
-        meridional_transit_ratio,
-        moisture_ratio,
-        stratum_depths,
-        sun_elevation_factor,
-        thermal_anomaly,
+        *hold(
+            zonal_transit_ratio,
+            meridional_transit_ratio,
+            moisture_ratio,
+            stratum_depths,
+            sun_elevation_factor,
+            thermal_anomaly,
+        ),
         *rims,
     )
     fields = lax.all_to_all(packed, "gy", split_axis=0, concat_axis=0, tiled=True)
@@ -551,7 +678,7 @@
         out_specs=(vmem, vmem),
         compiler_params=pltpu.CompilerParams(vmem_limit_bytes=4 * 1024 * 1024),
         name="turn",
-    )(fields, ground_cover_kind, particle_class_map)
+    )(fields, *hold(ground_cover_kind, particle_class_map))
 
     warmed = pl.pallas_call(
         warm_kernel,
@@ -561,23 +688,7 @@
         scratch_shapes=[pltpu.VMEM((tile + 16, LANES), f32)],
         compiler_params=pltpu.CompilerParams(vmem_limit_bytes=4 * 1024 * 1024),
         name="warm",
-    )(place, thermal_anomaly, *rims, fields)
-
-    whole = pl.pallas_call(
-        own_kernel,
-        out_shape=(
-            jax.ShapeDtypeStruct((levels, columns, LANES + 2 * MARGIN, species), bf16),
-            jax.ShapeDtypeStruct((FIELD_ROWS, LANES), f32),
-            jax.ShapeDtypeStruct((columns, LANES), jnp.int32),
-            jax.ShapeDtypeStruct((levels, LANES + 2 * MARGIN, LANES), bf16),
-        ),
-        in_specs=[smem, hbm] + [vmem] * 3,
-        out_specs=(vmem,) * 4,
-        scratch_shapes=[pltpu.SemaphoreType.DMA((3,))],
-        compiler_params=pltpu.CompilerParams(vmem_limit_bytes=4 * 1024 * 1024),
-        name="own",
-    )(place, tracer_amounts, fields, classes, turned)
-    own_inputs = [whole[1], whole[2], whole[3], whole[0]]
+    )(place, *hold(thermal_anomaly), *rims, fields)
 
     spread = jnp.asarray(spread_matrix(), bf16)
     table = jnp.concatenate([arid_extinction_table, swelling_factors], axis=1).T
@@ -589,58 +700,36 @@
     parts.append(jnp.zeros((LANES - 3 * settling_velocities.shape[0], species), bf16))
     speeds = jnp.concatenate(parts, axis=0)
 
+    coef_shape = (24, LANES + 2 * NEAR, LANES)
+    coefficients = pl.pallas_call(
+        coefficient_kernel,
+        out_shape=(
+            pltpu.HBM((gy, levels) + coef_shape, f32),
+            pltpu.HBM((gy, columns, LANES, LANES), f32),
+        ),
+        in_specs=[vmem] * 3,
+        out_specs=(hbm, hbm),
+        scratch_shapes=[
+            pltpu.VMEM((levels,) + coef_shape, f32),
+            pltpu.VMEM((columns, LANES, LANES), bf16),
+            pltpu.VMEM((columns, LANES, LANES), f32),
+            pltpu.SemaphoreType.DMA((levels,)),
+            pltpu.SemaphoreType.DMA((1,)),
+        ],
+        compiler_params=pltpu.CompilerParams(vmem_limit_bytes=12 * 1024 * 1024),
+        name="coefficients",
+    )(turned, spread, speeds)
+
     def run_chunk(k, out, heat):
-        first, final = k == 0, k == len(CHUNKS) - 1
-        operands = [place, arriving_irradiance, spread, table, speeds]
-        operands += own_inputs if final else [fields, classes, turned, tracer_amounts]
-        operands += halos[k]
-        specs = [smem, smem] + [vmem] * 9
-        heat_block = (levels * columns, LANES)
-        out_shapes = [jax.ShapeDtypeStruct(tracer_amounts.shape, f32)]
-        out_specs = [hbm]
-        aliases = {}
-        if not first:
-            operands += halos[k - 1]
-            specs += [vmem] * 2
-            if final:
-                operands += halos[0]
-                specs += [vmem] * 2
-            aliases[len(operands)] = 0
-            operands.append(out)
-            specs.append(hbm)
+        operands = [table, fields, classes]
+        final = k == len(CHUNKS) - 1
+        for n in [k] + [k - 1] * (k > 0) + [0] * final:
+            operands += halos[n]
         if final:
-            out_shapes.append(jax.ShapeDtypeStruct(heat_block, f32))
-            out_specs.append(vmem)
-        else:
-            if not first:
-                aliases[len(operands)] = 1
-                operands.append(heat)
-                specs.append(hbm)
-            out_shapes.append(jax.ShapeDtypeStruct((gy,) + heat_block, f32))
-            out_specs.append(hbm)
-        work = CHUNKS[k] * LANES * columns * levels * species
-        span = LANES + 2 * MARGIN
-        return pl.pallas_call(
-            functools.partial(chunk_kernel, k),
-            out_shape=tuple(out_shapes),
-            in_specs=specs,
-            out_specs=tuple(out_specs),
-            scratch_shapes=[
-                pltpu.VMEM((columns + 2 * SUB, span, LANES), f32),
-                pltpu.VMEM((columns + 2 * SUB, span, LANES), f32),
-                pltpu.VMEM((24, LANES + 2 * NEAR, LANES), f32),
-                pltpu.VMEM((2, levels, columns, LANES, LANES), f32),
-                pltpu.VMEM((columns, 8, LANES), f32),
-                pltpu.VMEM((2, levels * columns, LANES), f32),
-                pltpu.SemaphoreType.DMA((2, levels)),
-                pltpu.SemaphoreType.DMA((2,)),
-            ],
-            input_output_aliases=aliases,
-            compiler_params=pltpu.CompilerParams(vmem_limit_bytes=12 * 1024 * 1024),
-            cost_estimate=pl.CostEstimate(
-                flops=60 * work, transcendentals=0, bytes_accessed=8 * work
-            ),
-        )(*operands)
+            operands = hold(*operands)
+        held = hold(tracer_amounts, *coefficients)
+        operands = [place, arriving_irradiance] + operands[:3] + held + operands[3:]
+        return chunk_call(k, operands, out, heat, tracer_amounts.shape, gy)
 
     out = heat = None
     for k in range(len(CHUNKS) - 1):

time: 146 us -> 140 us (0.959)
  local copies, waits for them, and re-layouts: 17.9 us -> 0.83 us
  Pallas kernels: 50.5 us -> 67.4 us
  waiting for transfers between devices: 40 us -> 29.5 us
  starting transfers between devices: 31.9 us -> 38 us
  other arithmetic: 2.84 us -> 0.88 us
    unnamed x62 -> x26, local copies, waits for them, and re-layouts: 17.8 us -> 0.75 us
    pallas_call x6 -> x7, Pallas kernels: 46.7 us -> 61.3 us  [the longest x5 41.9 us: chunk_call(): pl.pallas_call(functools.partial(chunk_kernel, k), out_shape=tuple(out_sh...]
    all_to_all x1, waiting for transfers between devices: 11.2 us -> 0.01 us  [per_device(): lax.all_to_all(packed, 'gy', split_axis=0, concat_axis=0, tiled=True)]
    all_to_all x1, starting transfers between devices: 7.41 us -> 11.3 us  [per_device(): lax.all_to_all(packed, 'gy', split_axis=0, concat_axis=0, tiled=True)]
    ppermute x8 -> x10, starting transfers between devices: 12.9 us -> 16.2 us  [per_device(): lax.ppermute(h, strips, p)]
    ppermute x2, starting transfers between devices: 5.49 us -> 3.56 us  [per_device(): rims = [lax.ppermute(r, 'gx', p) for r, p in zip((rim_0, rim_1), swaps(gx))]]
    ppermute x8 -> x10, waiting for transfers between devices: 28.6 us -> 28.7 us  [per_device(): lax.ppermute(h, strips, p)]
  transfers between devices with their start and end apart: 12 -> 14, of which waited for: 4 -> 3; matrix products, arithmetic and copies ran while one was open for 1% -> 0% of each run, Pallas kernels for 34% -> 47%
where the time goes in v3:
time: 140 us; the launch traced here: 138 us
  Pallas kernels  67.4 us (48%)
  starting transfers between devices  38 us (27%)
  waiting for transfers between devices  29.5 us (21%)
    pallas_call x5, Pallas kernels, chunk_call(): pl.pallas_call(functools.partial(chunk_kernel, k), out_shape=tuple(out_sh...  41.9 us
    ppermute x10, waiting for transfers between devices, per_device(): lax.ppermute(h, strips, p)  28.7 us
    ppermute x10, starting transfers between devices, per_device(): lax.ppermute(h, strips, p)  16.2 us
    pallas_call x1, Pallas kernels, per_device(): pl.pallas_call(coefficient_kernel, out_shape=(pltpu.HBM((gy, levels) + co...  15.2 us
    all_to_all x1, starting transfers between devices, per_device(): lax.all_to_all(packed, 'gy', split_axis=0, concat_axis=0, tiled=True)  11.3 us
    all_to_all x1, starting transfers between devices, per_device(): lax.all_to_all(heat, 'gy', split_axis=0, concat_axis=0, tiled=True)  7.01 us
    pallas_call x1, Pallas kernels, per_device(): pl.pallas_call(later_slice_kernel, out_shape=tuple((pltpu.HBM(x.shape, x....  4.16 us
    ppermute x2, starting transfers between devices, per_device(): rims = [lax.ppermute(r, 'gx', p) for r, p in zip((rim_0, rim_1), swaps(gx))]  3.56 us
  transfers between devices with their start and end apart: 14, of which 3 were waited for; matrix products, arithmetic and copies ran while one was open for 0% of the time, Pallas kernels for 47%

profile of v3, /device:TPU:0, one launch (start us, length us, event | category | flops | bytes accessed | tf_op | source)
XLA Modules:
  0.0 137.7 jit_solution(5294281250934148734)
XLA Ops:
  0.8 2.2 %slice_first.1 = (bf16[2,3,160,128]{3,2,1,0:T(8,128)(2,1)S(1)}, bf16[2,3,160,128]{3,2,1,0:T(8,128)(2,1)S(1)}, f32[16,128]{1,0:T(8,128)S(1)}, f32[16,128]{1,0:T(8,128)S(1)}) custom-call(s32[3]{0:T(128)S(1)} %pad_add_fusion.place.refs_0_, bf16[2,8,1024,128]{3,2,1,0:T(8,128)(2,1)} %refs_5_.9, f32[2,64,128]{2,1,0:T(8,128)} %u.3, f32[2,64,128]{2,1,0:T(8,128)} %v.3, ...), custom_call_target="tpu_custom_call" | custom-call | tf_op jit(solution)/shard_map/slice_first/pallas_call | solution.py:613
  2.9 2.1 %collective-permute-start.6 = (bf16[2,3,160,128]{3,2,1,0:T(8,128)(2,1)S(1)}, bf16[2,3,160,128]{3,2,1,0:T(8,128)(2,1)S(1)}, u32[]{:S(2)}, u32[]{:S(2)}) collective-permute-start(bf16[2,3,160,128]{3,2,1,0:T(8,128)(2,1)S(1)} %get-tuple-element.38), channel_id=1, source_target_pairs={{0,1},{2,3},{4,5},{6,7},{8,9},{10,11},{12,13},{14,15},{16,17},{18,... | collective-permute-start | bytes 737288 | tf_op jit(solution)/shard_map/ppermute | solution.py:647
  5.0 4.2 %slice_later.1 = (bf16[2,3,384,128]{3,2,1,0:T(8,128)(2,1)}, bf16[2,3,384,128]{3,2,1,0:T(8,128)(2,1)}, bf16[2,3,256,128]{3,2,1,0:T(8,128)(2,1)}, bf16[2,3,256,128...) custom-call(s32[3]{0:T(128)S(1)} %pad_add_fusion.place.refs_0_, ...), custom_call_target="tpu_custom_call" | custom-call | tf_op jit(solution)/shard_map/slice_later/pallas_call | solution.py:628
  9.3 2.0 %collective-permute-start.10 = (bf16[2,3,384,128]{3,2,1,0:T(8,128)(2,1)}, bf16[2,3,384,128]{3,2,1,0:T(8,128)(2,1)S(1)}, u32[]{:S(2)}, u32[]{:S(2)}) collective-permute-start(bf16[2,3,384,128]{3,2,1,0:T(8,128)(2,1)} %get-tuple-element.42), channel_id=1, source_target_pairs={{0,1},{2,3},{4,5},{6,7},{8,9},{10,11},{12,13},{14,15},{16,17},{18,... | collective-permute-start | bytes 1769480 | tf_op jit(solution)/shard_map/ppermute | solution.py:647
  11.3 1.5 %collective-permute-start.11 = (bf16[2,3,384,128]{3,2,1,0:T(8,128)(2,1)}, bf16[2,3,384,128]{3,2,1,0:T(8,128)(2,1)}, u32[]{:S(2)}, u32[]{:S(2)}) collective-permute-start(bf16[2,3,384,128]{3,2,1,0:T(8,128)(2,1)} %get-tuple-element.43), channel_id=1, source_target_pairs={{1,2},{3,4},{5,6},{7,8},{9,10},{11,12},{13,14},{15,16},{17,18},{19... | collective-permute-start | bytes 1769480 | tf_op jit(solution)/shard_map/ppermute | solution.py:647
  12.8 2.9 %collective-permute-start = (f32[16,128]{1,0:T(8,128)S(1)}, f32[16,128]{1,0:T(8,128)S(1)}, u32[]{:S(2)}, u32[]{:S(2)}) collective-permute-start(f32[16,128]{1,0:T(8,128)S(1)} %get-tuple-element.28), channel_id=1, source_target_pairs={{0,8},{16,24},{32,40},{48,56},{64,72},{80,88},{96,104},{112,120},{... | collective-permute-start | bytes 24584 | tf_op jit(solution)/shard_map/ppermute | solution.py:643
  15.7 0.8 collective-permute-done.rim_0
  17.9 1.9 %pack.1 = f32[8,96,128]{2,1,0:T(8,128)} custom-call(s32[3]{0:T(128)S(1)} %pad_add_fusion.place.refs_0_, f32[2,64,128]{2,1,0:T(8,128)} %u.3, f32[2,64,128]{2,1,0:T(8,128)} %v.3, f32[2,64,128]{2,1,0:T(8,128)} %moisture.1, f32[2,64,128]{2,1,0:T(8,128)} %depth.1, f32[64,128]{1,0:T(8,128)} %sun.1, f32[2,64,128]{2,1,0:T(8,128)} %warmth.5, ...), custom_call_target="tpu_custom_call" | custom-call | tf_op jit(solution)/shard_map/pack/pallas_call | solution.py:649
  19.8 11.3 %all-to-all-start = ((f32[8,96,128]{2,1,0:T(8,128)}), f32[8,96,128]{2,1,0:T(8,128)S(1)}, u32[]{:S(2)}, u32[]{:S(2)}) async-start(f32[8,96,128]{2,1,0:T(8,128)} %pack.1), calls=%async_computation | async-start | bytes 786432 | tf_op jit(solution)/shard_map/all_to_all | solution.py:669
  31.0 1.4 %collective-permute-start.9 = (bf16[2,3,256,128]{3,2,1,0:T(8,128)(2,1)}, bf16[2,3,256,128]{3,2,1,0:T(8,128)(2,1)}, u32[]{:S(2)}, u32[]{:S(2)}) collective-permute-start(bf16[2,3,256,128]{3,2,1,0:T(8,128)(2,1)} %get-tuple-element.41), channel_id=1, source_target_pairs={{1,2},{3,4},{5,6},{7,8},{9,10},{11,12},{13,14},{15,16},{17,18},{19... | collective-permute-start | bytes 1179656 | tf_op jit(solution)/shard_map/ppermute | solution.py:647
  32.6 4.0 %collective-permute-start.4 = (bf16[2,3,128,128]{3,2,1,0:T(8,128)(2,1)}, bf16[2,3,128,128]{3,2,1,0:T(8,128)(2,1)S(1)}, u32[]{:S(2)}, u32[]{:S(2)}) collective-permute-start(bf16[2,3,128,128]{3,2,1,0:T(8,128)(2,1)} %get-tuple-element.36), channel_id=1, source_target_pairs={{0,1},{2,3},{4,5},{6,7},{8,9},{10,11},{12,13},{14,15},{16,17},{18,... | collective-permute-start | bytes 589832 | tf_op jit(solution)/shard_map/ppermute | solution.py:647
  36.6 12.6 %collective-permute-done.8.refs_8_.refs_10_ = bf16[2,3,256,128]{3,2,1,0:T(8,128)(2,1)} collective-permute-done((bf16[2,3,256,128]{3,2,1,0:T(8,128)(2,1)}, bf16[2,3,256,128]{3,2,1,0:T(8,128)(2,1)}, u32[]{:S(2)}, u32[]{:S(2)}) %collective-permute-start.8) | collective-permute-done | bytes 393248 | tf_op jit(solution)/shard_map/ppermute | solution.py:647
  49.9 16.1 %collective-permute-done.10.refs_8_.refs_10_ = bf16[2,3,384,128]{3,2,1,0:T(8,128)(2,1)S(1)} collective-permute-done((bf16[2,3,384,128]{3,2,1,0:T(8,128)(2,1)}, bf16[2,3,384,128]{3,2,1,0:T(8,128)(2,1)S(1)}, u32[]{:S(2)}, u32[]{:S(2)}) %collective-permute-start.10) | collective-permute-done | bytes 589856 | tf_op jit(solution)/shard_map/ppermute | solution.py:647
  66.0 2.4 %collective-permute-start.2 = (bf16[2,3,112,128]{3,2,1,0:T(8,128)(2,1)}, bf16[2,3,112,128]{3,2,1,0:T(8,128)(2,1)}, u32[]{:S(2)}, u32[]{:S(2)}) collective-permute-start(bf16[2,3,112,128]{3,2,1,0:T(8,128)(2,1)} %get-tuple-element.34), channel_id=1, source_target_pairs={{0,1},{2,3},{4,5},{6,7},{8,9},{10,11},{12,13},{14,15},{16,17},{18,... | collective-permute-start | bytes 516104 | tf_op jit(solution)/shard_map/ppermute | solution.py:647
  68.4 1.3 collective-permute-start.3
  69.7 1.0 turn.1
  70.8 15.2 %coefficients.1 = (f32[8,2,24,144,128]{4,3,2,1,0:T(8,128)}, f32[8,8,128,128]{3,2,1,0:T(8,128)}) custom-call(bf16[2,8,128,128]{3,2,1,0:T(8,128)(2,1)S(1)} %get-tuple-element.31.turned, bf16[20,128,256]{2,1,0:T(8,128)(2,1)S(1)} %copy-done.3, bf16[128,128]{1,0:T(8,128)(2,1)S(1)} %maximum_maximum_fusion.speeds), custom_call_target="tpu_custom_call" | custom-call | tf_op jit(solution)/shard_map/coefficients/pallas_call | solution.py:704
  86.1 6.4 %shard_map.149 = (f32[2,8,1024,128]{3,2,1,0:T(8,128)}, f32[8,16,128]{2,1,0:T(8,128)}) custom-call(s32[3]{0:T(128)S(1)} %pad_add_fusion.place.refs_0_, f32[4]{0:T(128)S(1)} %copy-done.6, bf16[128,128]{1,0:T(8,128)(2,1)S(1)} %maximum_bitcast_fusion.refs_2_, f32[8,96,128]{2,1,0:T(8,128)S(1)} %all-to-all-done.fields.refs_3_, ...), custom_call_target="tpu_custom_call" | custom-call | flops 15728640 | bytes 2097152 | tf_op jit(solution)/shard_map/pallas_call | solution.py:550
  92.5 12.6 %shard_map.150 = (f32[2,8,1024,128]{3,2,1,0:T(8,128)}, f32[8,16,128]{2,1,0:T(8,128)}) custom-call(s32[3]{0:T(128)S(1)} %pad_add_fusion.place.refs_0_, f32[4]{0:T(128)S(1)} %copy-done.6, bf16[128,128]{1,0:T(8,128)(2,1)S(1)} %maximum_bitcast_fusion.refs_2_, ...), custom_call_target="tpu_custom_call", output_to_operand_aliasing={{0}: (12, {}), {1}: (13, {})} | custom-call | flops 47185920 | bytes 6291456 | tf_op jit(solution)/shard_map/pallas_call | solution.py:550
  105.1 9.8 %shard_map.151 = (f32[2,8,1024,128]{3,2,1,0:T(8,128)}, f32[8,16,128]{2,1,0:T(8,128)}) custom-call(s32[3]{0:T(128)S(1)} %pad_add_fusion.place.refs_0_, f32[4]{0:T(128)S(1)} %copy-done.6, bf16[128,128]{1,0:T(8,128)(2,1)S(1)} %maximum_bitcast_fusion.refs_2_, ...), custom_call_target="tpu_custom_call", output_to_operand_aliasing={{0}: (12, {}), {1}: (13, {})} | custom-call | flops 31457280 | bytes 4194304 | tf_op jit(solution)/shard_map/pallas_call | solution.py:550
  115.7 6.6 %shard_map.152 = (f32[2,8,1024,128]{3,2,1,0:T(8,128)}, f32[8,16,128]{2,1,0:T(8,128)}) custom-call(s32[3]{0:T(128)S(1)} %pad_add_fusion.place.refs_0_, f32[4]{0:T(128)S(1)} %copy-done.6, bf16[128,128]{1,0:T(8,128)(2,1)S(1)} %maximum_bitcast_fusion.refs_2_, ...), custom_call_target="tpu_custom_call", output_to_operand_aliasing={{0}: (12, {}), {1}: (13, {})} | custom-call | flops 15728640 | bytes 2097152 | tf_op jit(solution)/shard_map/pallas_call | solution.py:550
  122.2 7.0 %all-to-all-start.1 = ((f32[8,16,128]{2,1,0:T(8,128)}), f32[8,16,128]{2,1,0:T(8,128)S(1)}, u32[]{:S(2)}, u32[]{:S(2)}) async-start(f32[8,16,128]{2,1,0:T(8,128)} %get-tuple-element.53), calls=%async_computation.1 | async-start | bytes 131072 | tf_op jit(solution)/shard_map/all_to_all | solution.py:737
  129.3 1.1 warm.1
  130.4 6.6 %shard_map.153 = (f32[2,8,1024,128]{3,2,1,0:T(8,128)}, f32[16,128]{1,0:T(8,128)S(1)}) custom-call(s32[3]{0:T(128)S(1)} %pad_add_fusion.place.refs_0_, f32[4]{0:T(128)S(1)} %copy-done.6, bf16[128,128]{1,0:T(8,128)(2,1)} %copy-done.4, f32[8,96,128]{2,1,0:T(8,128)} %copy-done, s32[8,8,128]{2,1,0:T(8,128)} %copy-done.5, ...), custom_call_target="tpu_custom_call", output_to_operand_aliasing={{0}: (14, {})} | custom-call | flops 15728640 | bytes 2097152 | tf_op jit(solution)/shard_map/pallas_call | solution.py:550
  (49 shorter events, 3.8 us)
Async XLA Ops:
  0.6 70.2 %copy-start.3 = (bf16[20,128,256]{2,1,0:T(8,128)(2,1)S(1)}, bf16[20,128,256]{2,1,0:T(8,128)(2,1)}, u32[]{:S(2)}) copy-start(bf16[20,128,256]{2,1,0:T(8,128)(2,1)} %constant.20.clone.spread) | copy-start | bytes 3932164
  0.6 31.8 %copy-start.12 = (f32[24,128]{1,0:T(8,128)S(1)}, f32[24,128]{1,0:T(8,128)}, u32[]{:S(2)}) copy-start(f32[24,128]{1,0:T(8,128)} %param.25) | copy-start | bytes 36868
  0.7 69.1 %copy-start.10 = (bf16[128,64]{0,1:T(8,128)(2,1)S(1)}, bf16[128,64]{0,1:T(8,128)(2,1)}, u32[]{:S(2)}) copy-start(bf16[128,64]{0,1:T(8,128)(2,1)} %param.24) | copy-start | bytes 49156
  0.7 69.0 %copy-start.11 = (bf16[128,64]{0,1:T(8,128)(2,1)S(1)}, bf16[128,64]{0,1:T(8,128)(2,1)}, u32[]{:S(2)}) copy-start(bf16[128,64]{0,1:T(8,128)(2,1)} %param.23) | copy-start | bytes 49156
  0.7 85.4 %copy-start.6 = (f32[4]{0:T(128)S(1)}, f32[4]{0:T(128)}, u32[]{:S(2)}) copy-start(f32[4]{0:T(128)} %refs_1_.9) | copy-start | bytes 52
  2.9 28.1 %collective-permute-start.6 = (bf16[2,3,160,128]{3,2,1,0:T(8,128)(2,1)S(1)}, bf16[2,3,160,128]{3,2,1,0:T(8,128)(2,1)S(1)}, u32[]{:S(2)}, u32[]{:S(2)}) collective-permute-start(bf16[2,3,160,128]{3,2,1,0:T(8,128)(2,1)S(1)} %get-tuple-element.38), channel_id=1, source_target_pairs={{0,1},{2,3},{4,5},{6,7},{8,9},{10,11},{12,13},{14,15},{16,17},{18,... | collective-permute-start | bytes 737288 | tf_op jit(solution)/shard_map/ppermute | solution.py:647
  9.2 39.9 %collective-permute-start.8 = (bf16[2,3,256,128]{3,2,1,0:T(8,128)(2,1)}, bf16[2,3,256,128]{3,2,1,0:T(8,128)(2,1)}, u32[]{:S(2)}, u32[]{:S(2)}) collective-permute-start(bf16[2,3,256,128]{3,2,1,0:T(8,128)(2,1)} %get-tuple-element.40), channel_id=1, source_target_pairs={{0,1},{2,3},{4,5},{6,7},{8,9},{10,11},{12,13},{14,15},{16,17},{18,... | collective-permute-start | bytes 1179656 | tf_op jit(solution)/shard_map/ppermute | solution.py:647
  9.3 56.7 %collective-permute-start.10 = (bf16[2,3,384,128]{3,2,1,0:T(8,128)(2,1)}, bf16[2,3,384,128]{3,2,1,0:T(8,128)(2,1)S(1)}, u32[]{:S(2)}, u32[]{:S(2)}) collective-permute-start(bf16[2,3,384,128]{3,2,1,0:T(8,128)(2,1)} %get-tuple-element.42), channel_id=1, source_target_pairs={{0,1},{2,3},{4,5},{6,7},{8,9},{10,11},{12,13},{14,15},{16,17},{18,... | collective-permute-start | bytes 1769480 | tf_op jit(solution)/shard_map/ppermute | solution.py:647
  11.3 57.1 %collective-permute-start.11 = (bf16[2,3,384,128]{3,2,1,0:T(8,128)(2,1)}, bf16[2,3,384,128]{3,2,1,0:T(8,128)(2,1)}, u32[]{:S(2)}, u32[]{:S(2)}) collective-permute-start(bf16[2,3,384,128]{3,2,1,0:T(8,128)(2,1)} %get-tuple-element.43), channel_id=1, source_target_pairs={{1,2},{3,4},{5,6},{7,8},{9,10},{11,12},{13,14},{15,16},{17,18},{19... | collective-permute-start | bytes 1769480 | tf_op jit(solution)/shard_map/ppermute | solution.py:647
  12.8 3.7 %collective-permute-start = (f32[16,128]{1,0:T(8,128)S(1)}, f32[16,128]{1,0:T(8,128)S(1)}, u32[]{:S(2)}, u32[]{:S(2)}) collective-permute-start(f32[16,128]{1,0:T(8,128)S(1)} %get-tuple-element.28), channel_id=1, source_target_pairs={{0,8},{16,24},{32,40},{48,56},{64,72},{80,88},{96,104},{112,120},{... | collective-permute-start | bytes 24584 | tf_op jit(solution)/shard_map/ppermute | solution.py:643
  16.5 0.7 collective-permute-start.1
  17.2 15.4 %collective-permute-start.7 = (bf16[2,3,160,128]{3,2,1,0:T(8,128)(2,1)S(1)}, bf16[2,3,160,128]{3,2,1,0:T(8,128)(2,1)S(1)}, u32[]{:S(2)}, u32[]{:S(2)}) collective-permute-start(bf16[2,3,160,128]{3,2,1,0:T(8,128)(2,1)S(1)} %get-tuple-element.39), channel_id=1, source_target_pairs={{1,2},{3,4},{5,6},{7,8},{9,10},{11,12},{13,14},{15,16},{17,18},{19... | collective-permute-start | bytes 737288 | tf_op jit(solution)/shard_map/ppermute | solution.py:647
  19.8 50.0 %all-to-all-start = ((f32[8,96,128]{2,1,0:T(8,128)}), f32[8,96,128]{2,1,0:T(8,128)S(1)}, u32[]{:S(2)}, u32[]{:S(2)}) async-start(f32[8,96,128]{2,1,0:T(8,128)} %pack.1), calls=%async_computation | async-start | bytes 786432 | tf_op jit(solution)/shard_map/all_to_all | solution.py:669
  31.0 61.5 %copy-start.1 = (bf16[2,3,160,128]{3,2,1,0:T(8,128)(2,1)}, bf16[2,3,160,128]{3,2,1,0:T(8,128)(2,1)S(1)}, u32[]{:S(2)}) copy-start(bf16[2,3,160,128]{3,2,1,0:T(8,128)(2,1)S(1)} %collective-permute-done.6.refs_8_.refs_10_.refs_12_) | copy-start | bytes 737284
  31.0 74.1 %collective-permute-start.9 = (bf16[2,3,256,128]{3,2,1,0:T(8,128)(2,1)}, bf16[2,3,256,128]{3,2,1,0:T(8,128)(2,1)}, u32[]{:S(2)}, u32[]{:S(2)}) collective-permute-start(bf16[2,3,256,128]{3,2,1,0:T(8,128)(2,1)} %get-tuple-element.41), channel_id=1, source_target_pairs={{1,2},{3,4},{5,6},{7,8},{9,10},{11,12},{13,14},{15,16},{17,18},{19... | collective-permute-start | bytes 1179656 | tf_op jit(solution)/shard_map/ppermute | solution.py:647
  32.6 59.9 %copy-start.2 = (bf16[2,3,160,128]{3,2,1,0:T(8,128)(2,1)}, bf16[2,3,160,128]{3,2,1,0:T(8,128)(2,1)S(1)}, u32[]{:S(2)}) copy-start(bf16[2,3,160,128]{3,2,1,0:T(8,128)(2,1)S(1)} %collective-permute-done.7.refs_9_.refs_11_.refs_13_) | copy-start | bytes 737284
  32.6 82.3 %collective-permute-start.4 = (bf16[2,3,128,128]{3,2,1,0:T(8,128)(2,1)}, bf16[2,3,128,128]{3,2,1,0:T(8,128)(2,1)S(1)}, u32[]{:S(2)}, u32[]{:S(2)}) collective-permute-start(bf16[2,3,128,128]{3,2,1,0:T(8,128)(2,1)} %get-tuple-element.36), channel_id=1, source_target_pairs={{0,1},{2,3},{4,5},{6,7},{8,9},{10,11},{12,13},{14,15},{16,17},{18,... | collective-permute-start | bytes 589832 | tf_op jit(solution)/shard_map/ppermute | solution.py:647
  49.1 65.8 %collective-permute-start.5 = (bf16[2,3,128,128]{3,2,1,0:T(8,128)(2,1)}, bf16[2,3,128,128]{3,2,1,0:T(8,128)(2,1)S(1)}, u32[]{:S(2)}, u32[]{:S(2)}) collective-permute-start(bf16[2,3,128,128]{3,2,1,0:T(8,128)(2,1)} %get-tuple-element.37), channel_id=1, source_target_pairs={{1,2},{3,4},{5,6},{7,8},{9,10},{11,12},{13,14},{15,16},{17,18},{19... | collective-permute-start | bytes 589832 | tf_op jit(solution)/shard_map/ppermute | solution.py:647
  66.0 64.4 %collective-permute-start.2 = (bf16[2,3,112,128]{3,2,1,0:T(8,128)(2,1)}, bf16[2,3,112,128]{3,2,1,0:T(8,128)(2,1)}, u32[]{:S(2)}, u32[]{:S(2)}) collective-permute-start(bf16[2,3,112,128]{3,2,1,0:T(8,128)(2,1)} %get-tuple-element.34), channel_id=1, source_target_pairs={{0,1},{2,3},{4,5},{6,7},{8,9},{10,11},{12,13},{14,15},{16,17},{18,... | collective-permute-start | bytes 516104 | tf_op jit(solution)/shard_map/ppermute | solution.py:647
  68.4 62.0 %collective-permute-start.3 = (bf16[2,3,112,128]{3,2,1,0:T(8,128)(2,1)}, bf16[2,3,112,128]{3,2,1,0:T(8,128)(2,1)}, u32[]{:S(2)}, u32[]{:S(2)}) collective-permute-start(bf16[2,3,112,128]{3,2,1,0:T(8,128)(2,1)} %get-tuple-element.35), channel_id=1, source_target_pairs={{1,2},{3,4},{5,6},{7,8},{9,10},{11,12},{13,14},{15,16},{17,18},{19... | collective-permute-start | bytes 516104 | tf_op jit(solution)/shard_map/ppermute | solution.py:647
  69.7 45.2 %copy-start.4 = (bf16[128,128]{1,0:T(8,128)(2,1)}, bf16[128,128]{1,0:T(8,128)(2,1)S(1)}, u32[]{:S(2)}) copy-start(bf16[128,128]{1,0:T(8,128)(2,1)S(1)} %maximum_bitcast_fusion.refs_2_) | copy-start | bytes 98308
  69.7 59.5 %copy-start = (f32[8,96,128]{2,1,0:T(8,128)}, f32[8,96,128]{2,1,0:T(8,128)S(1)}, u32[]{:S(2)}) copy-start(f32[8,96,128]{2,1,0:T(8,128)S(1)} %all-to-all-done.fields.refs_3_) | copy-start | bytes 1179652
  70.8 44.2 %copy-start.5 = (s32[8,8,128]{2,1,0:T(8,128)}, s32[8,8,128]{2,1,0:T(8,128)S(1)}, u32[]{:S(2)}) copy-start(s32[8,8,128]{2,1,0:T(8,128)S(1)} %get-tuple-element.30.refs_4_) | copy-start | bytes 98308
  122.2 14.7 %all-to-all-start.1 = ((f32[8,16,128]{2,1,0:T(8,128)}), f32[8,16,128]{2,1,0:T(8,128)S(1)}, u32[]{:S(2)}, u32[]{:S(2)}) async-start(f32[8,16,128]{2,1,0:T(8,128)} %get-tuple-element.53), calls=%async_computation.1 | async-start | bytes 131072 | tf_op jit(solution)/shard_map/all_to_all | solution.py:737
  (3 other events, 27.9 us)
